TPU v7x, 512 devices: a whole 4x4x16 slice. The times are simulated.
512 devices in a mesh: rep: 2 (over core), row: 32 (over x_hi, z), col: 8 (over x_lo, y).
Axes of the slice: x: 4 (x_hi: 2, x_lo: 2; x = x_hi * 2 + x_lo), y: 4, z: 16, core: 2. Of those that a mesh axis runs over, the one named last changes fastest.
Arguments:
- sources: float32 [2, 384, 384, 384], P('rep', 'col', 'row'), may hold values from -6 to 6
Outputs:
- potential: float32 [384, 384, 384], P(('rep', 'col'), 'row')
All inputs are finite; a program needn't handle non-finite values.
Results may differ from a plain program's by a relative error of at most 0.000096.
Values sent between devices are 32-bit elements; how exact they have to be, the bound alone decides.
No kernel may reach another device: no remote copies, remote signals or barrier semaphores. Data moves between devices by JAX's collectives and lax.ppermute only.
A program may use at most 64 MiB of HBM per device.

v0:
```python
import numpy as np

import jax
import jax.numpy as jnp
from jax import lax
from jax.sharding import PartitionSpec as P

N = 384
SHIFT = 0.001


def hartley_table():
    turns = np.outer(np.arange(N), np.arange(N)) % N
    angle = turns * (2.0 * np.pi / N)
    return (np.cos(angle) + np.sin(angle)).astype(np.float32)


def eigen_line():
    return (4.0 * np.sin(np.pi * np.arange(N) / N) ** 2).astype(np.float32)


def dot3(a, b, dims):
    return lax.dot_general(a, b, (dims, ((), ())), precision=lax.Precision.HIGH,
                           preferred_element_type=jnp.float32)


def body(sources):
    rep, col, row = lax.axis_index("rep"), lax.axis_index("col"), lax.axis_index("row")
    n_rep, n_col, n_row = lax.axis_size("rep"), lax.axis_size("col"), lax.axis_size("row")
    group = n_rep * n_col
    table = jnp.asarray(hartley_table())
    part = sources[0]
    nb = part.shape[1]
    na = part.shape[0] // n_rep
    ns = N // group
    halves = part.reshape(n_rep, na, nb, N)
    mine = lax.dynamic_index_in_dim(halves, rep, 0, keepdims=False)
    other = lax.dynamic_index_in_dim(halves, 1 - rep, 0, keepdims=False)
    density = mine + lax.ppermute(other, "rep", [(0, 1), (1, 0)])
    modes = dot3(density.reshape(na * nb, N), table, ((1,), (0,)))
    modes = modes.reshape(na, nb, group, ns).transpose(2, 0, 1, 3)
    modes = lax.all_to_all(modes.reshape(group, 1, na * nb * ns), ("rep", "col"), 0, 0, tiled=True)
    lines = modes.reshape(N, nb * ns)
    table_in = table.reshape(n_col, n_rep, na, N).transpose(1, 0, 2, 3).reshape(N, N)
    field = dot3(lines, table_in, ((0,), (0,))).reshape(nb, ns, N)
    eig = jnp.asarray(eigen_line())
    third = lax.dynamic_slice_in_dim(eig, (rep * n_col + col) * ns, ns)
    lam = third[:, None] + eig[None, :] + SHIFT
    root = jnp.sqrt(lam * (lam + 4.0))
    ratio = 2.0 / (2.0 + lam + root)
    powers = [jnp.ones_like(ratio)]
    for _ in range(nb):
        powers.append(powers[-1] * ratio)
    right = field[0]
    for i in range(1, nb):
        right = right * ratio + field[i]
    left = field[nb - 1]
    for i in range(nb - 2, -1, -1):
        left = left * ratio + field[i]
    waves = jnp.stack([right, left]).reshape(n_row, 1, 2 * ns * N // n_row)
    waves = lax.all_to_all(waves, "row", 0, 0, tiled=True)
    step = jnp.broadcast_to(powers[nb], (2, ns, N)).reshape(n_row, 1, 2 * ns * N // n_row)
    step = lax.dynamic_index_in_dim(step, row, 0, keepdims=True)
    per = 2 * ns * N // n_row
    chunks = waves.reshape(n_row, per)
    step = step.reshape(1, per)
    is_right = lax.broadcasted_iota(jnp.int32, (1, per), 1) + row * per < ns * N
    reach = 1
    while reach < n_row:
        back = jnp.roll(chunks, reach, 0)
        ahead = jnp.roll(chunks, -reach, 0)
        chunks = chunks + step * jnp.where(is_right, back, ahead)
        step = step * step
        reach *= 2
    chunks = chunks / (1.0 - step)
    chunks = jnp.where(is_right, jnp.roll(chunks, 1, 0), jnp.roll(chunks, -1, 0))
    waves = lax.all_to_all(chunks.reshape(n_row, 1, per), "row", 0, 0, tiled=True)
    waves = waves.reshape(2, ns, N)
    scale = (1.0 / (N * N)) / root
    run = waves[0]
    forward = []
    for i in range(nb):
        run = run * ratio
        forward.append(run)
        run = run + field[i]
    run = waves[1]
    result = [None] * nb
    for i in range(nb - 1, -1, -1):
        run = run * ratio + field[i]
        result[i] = (forward[i] + run) * scale
    result = jnp.stack(result)
    lines = dot3(table, result.reshape(nb * ns, N), ((0,), (1,)))
    lines = lax.all_to_all(lines.reshape(group, 1, na * nb * ns), ("rep", "col"), 0, 0, tiled=True)
    modes = lines.reshape(group, na, nb, ns).transpose(1, 2, 0, 3).reshape(na * nb, N)
    return dot3(modes, table, ((1,), (0,))).reshape(na, nb, N)


def solution(mesh):
    return jax.shard_map(
        body,
        mesh=mesh,
        in_specs=(P("rep", "col", "row", None),),
        out_specs=P(("rep", "col"), "row", None),
        check_vma=False,
    )
```

profile of v0, /device:TPU:1, one launch (start us, length us, event | category | flops | bytes accessed | tf_op | source)
XLA Modules:
  0.0 113.8 jit_solution(1686144901951031443)
XLA Ops:
  0.0 1.0 dynamic-slice_bitcast_fusion
  1.0 8.7 %collective-permute-start = (f32[24,12,384]{2,0,1:T(8,128)S(1)}, f32[24,12,384]{2,0,1:T(8,128)S(1)}, u32[]{:S(2)}, u32[]{:S(2)}) collective-permute-start(f32[24,12,384]{2,0,1:T(8,128)S(1)} %dynamic-slice_bitcast_fusion), channel_id=1, source_target_pairs={{0,256},{256,0},{1,257},{257,1},{2,258},{258,2},{3,259},{259,3},{4... | collective-permute-start | bytes 1327112 | tf_op jit(solution)/shard_map/ppermute | solution.py:39
  9.8 1.4 %collective-permute-done = f32[24,12,384]{2,0,1:T(8,128)S(1)} collective-permute-done((f32[24,12,384]{2,0,1:T(8,128)S(1)}, f32[24,12,384]{2,0,1:T(8,128)S(1)}, u32[]{:S(2)}, u32[]{:S(2)}) %collective-permute-start) | collective-permute-done | bytes 442400 | tf_op jit(solution)/shard_map/ppermute | solution.py:39
  11.2 3.2 %convolution_bitcast_fusion = f32[16,24,12,24]{3,1,0,2:T(8,128)S(1)} fusion(f32[16,24,384,1]{2,1,0,3:T(8,128)} %constant.68, f32[24,12,384]{2,0,1:T(8,128)S(1)} %collective-permute-done, f32[2,24,12,384]{3,1,0,2:T(8,128)} %bitcast.78, s32[]{:T(128)S(6)} %select_n.38), kind=kOutput, calls=%fused_computation | convolution fusion | flops 254914560 | bytes 1916932 | tf_op jit(solution)/shard_map/dot_general | solution.py:23
  14.4 1.4 %copy.7 = f32[16,24,12,24]{3,2,1,0:T(8,128)S(1)} copy(f32[16,24,12,24]{3,1,0,2:T(8,128)S(1)} %convolution_bitcast_fusion) | data formatting | bytes 884736 | tf_op jit(solution)/shard_map/transpose | solution.py:41
  15.9 0.0 copy-start.3
  15.9 2.6 %reshape.200 = f32[16,1,6912]{2,1,0:T(1,128)} reshape(f32[16,24,12,24]{3,2,1,0:T(8,128)S(1)} %copy.7) | data formatting | bytes 884736 | tf_op jit(solution)/shard_map/reshape | solution.py:42
  18.5 0.0 copy-start.1
  18.5 3.9 %all-to-all-start = ((f32[16,1,6912]{2,1,0:T(1,128)}), f32[16,1,6912]{2,1,0:T(1,128)S(1)}, u32[]{:S(2)}, u32[]{:S(2)}) async-start(f32[16,1,6912]{2,1,0:T(1,128)} %reshape.200), calls=%async_computation | async-start | bytes 884736 | tf_op jit(solution)/shard_map/all_to_all | solution.py:42
  22.4 0.0 copy-done.3
  22.4 0.1 dynamic_slice.16
  22.4 9.6 %all-to-all-done = f32[16,1,6912]{2,1,0:T(1,128)S(1)} async-done(((f32[16,1,6912]{2,1,0:T(1,128)}), f32[16,1,6912]{2,1,0:T(1,128)S(1)}, u32[]{:S(2)}, u32[]{:S(2)}) %all-to-all-start) | async-done | bytes 442400 | tf_op jit(solution)/shard_map/all_to_all | solution.py:42
  32.0 1.0 reduce
  33.1 0.4 reshape.188
  33.5 0.0 copy-done.1
  33.5 0.7 fusion.28
  34.2 0.1 multiply_multiply_fusion
  34.4 0.1 add_bitcast_fusion
  34.5 0.8 reshape.201
  35.3 14.0 %all-to-all-start.1 = ((f32[32,1,576]{2,1,0:T(1,128)}), f32[32,1,576]{2,1,0:T(1,128)S(1)}, u32[]{:S(2)}, u32[]{:S(2)}) async-start(f32[32,1,576]{2,1,0:T(1,128)} %reshape.201), calls=%async_computation.1 | async-start | bytes 163840 | tf_op jit(solution)/shard_map/all_to_all | solution.py:61
  49.3 0.1 reshape.193
  49.5 15.0 %all-to-all-done.1 = f32[32,1,576]{2,1,0:T(1,128)S(1)} async-done(((f32[32,1,576]{2,1,0:T(1,128)}), f32[32,1,576]{2,1,0:T(1,128)S(1)}, u32[]{:S(2)}, u32[]{:S(2)}) %all-to-all-start.1) | async-done | bytes 73760 | tf_op jit(solution)/shard_map/all_to_all | solution.py:61
  64.4 0.1 fusion.27
  64.8 0.0 copy-start
  64.9 0.1 copy.11
  65.0 18.4 %all_to_all.20 = f32[32,1,576]{2,1,0:T(1,128)S(1)} all-to-all(f32[32,1,576]{2,1,0:T(1,128)S(1)} %copy.11), channel_id=1, replica_groups=mesh['rep'=2,'row'=32,'col'=8] {'row'}, dimensions={0} | all-to-all | bytes 147456 | tf_op jit(solution)/shard_map/all_to_all | solution.py:77
  83.5 0.2 slice_reduce_fusion
  83.7 0.1 squeeze.13
  83.8 0.1 squeeze.14
  83.9 0.1 bitcast_dynamic-update-slice_fusion.11
  84.0 0.1 bitcast_dynamic-update-slice_fusion.10
  84.1 0.1 bitcast_dynamic-update-slice_fusion.9
  84.2 0.1 bitcast_dynamic-update-slice_fusion.8
  84.4 0.1 bitcast_dynamic-update-slice_fusion.7
  84.5 0.1 bitcast_dynamic-update-slice_fusion.6
  84.6 0.1 bitcast_dynamic-update-slice_fusion.5
  84.7 0.1 bitcast_dynamic-update-slice_fusion.4
  84.8 0.1 bitcast_dynamic-update-slice_fusion.3
  84.9 0.1 bitcast_dynamic-update-slice_fusion.2
  85.0 0.1 bitcast_dynamic-update-slice_fusion.1
  85.1 0.1 bitcast_dynamic-update-slice_fusion
  85.3 0.0 copy-done
  85.3 1.1 fusion.29
  86.4 0.8 reshape.202
  87.2 15.1 %all_to_all.21 = f32[16,1,6912]{2,1,0:T(1,128)S(1)} all-to-all(f32[16,1,6912]{2,1,0:T(1,128)S(1)} %reshape.202), channel_id=1, replica_groups=mesh['rep'=2,'row'=32,'col'=8] {'rep','col'}, dimensions={0} | all-to-all | bytes 884736 | tf_op jit(solution)/shard_map/all_to_all | solution.py:93
  102.3 1.9 %reduce.4 = f32[16,6912]{1,0:T(8,128)} reduce(f32[16,1,6912]{2,1,0:T(1,128)S(1)} %all_to_all.21, f32[]{:T(128)} %constant.70), dimensions={1}, to_apply=%all_to_all.15.reduce_sub_computation | reduce | bytes 884740 | tf_op jit(solution)/shard_map/all_to_all | solution.py:93
  104.2 2.7 %reshape.196 = f32[16,24,12,24]{3,2,1,0:T(8,128)S(1)} reshape(f32[16,6912]{1,0:T(8,128)} %reduce.4) | data formatting | bytes 884736 | tf_op jit(solution)/shard_map/reshape | solution.py:94
  106.9 2.8 %copy.14 = f32[24,12,16,24]{3,2,0,1:T(8,128)} copy(f32[24,12,16,24]{3,1,0,2:T(8,128)S(1)} %bitcast.76) | data formatting | bytes 884736 | tf_op jit(solution)/shard_map/transpose | solution.py:94
  109.7 0.0 copy-start.2
  109.7 2.7 %dot_general.26 = f32[24,12,384]{2,0,1:T(8,128)S(1)} reshape(f32[24,12,16,24]{3,2,0,1:T(8,128)} %copy.14) | data formatting | bytes 884736 | tf_op jit(solution)/shard_map/dot_general | solution.py:23
  112.4 0.0 copy-done.2
  112.4 1.3 %fusion.30 = f32[24,12,384]{2,0,1:T(8,128)} fusion(f32[24,12,384]{2,0,1:T(8,128)S(1)} %dot_general.26, f32[384,384,1]{1,0,2:T(8,128)S(1)} %copy-done.2), kind=kOutput, calls=%fused_computation.94 | convolution fusion | flops 254803968 | bytes 1474560 | tf_op jit(solution)/shard_map/dot_general | solution.py:23
  (22 shorter events, 0.3 us)
Async XLA Ops:
  1.0 10.2 %collective-permute-start = (f32[24,12,384]{2,0,1:T(8,128)S(1)}, f32[24,12,384]{2,0,1:T(8,128)S(1)}, u32[]{:S(2)}, u32[]{:S(2)}) collective-permute-start(f32[24,12,384]{2,0,1:T(8,128)S(1)} %dynamic-slice_bitcast_fusion), channel_id=1, source_target_pairs={{0,256},{256,0},{1,257},{257,1},{2,258},{258,2},{3,259},{259,3},{4... | collective-permute-start | bytes 1327112 | tf_op jit(solution)/shard_map/ppermute | solution.py:39
  15.9 6.5 %copy-start.3 = (f32[384]{0:T(512)S(1)}, f32[384]{0:T(512)}, u32[]{:S(2)}) copy-start(f32[384]{0:T(512)} %constant.61.clone) | copy-start | bytes 4612
  18.5 15.1 %copy-start.1 = (f32[384,384]{1,0:T(8,128)S(1)}, f32[384,384]{1,0:T(8,128)}, u32[]{:S(2)}) copy-start(f32[384,384]{1,0:T(8,128)} %constant.67) | copy-start | bytes 1769476
  18.5 13.6 %all-to-all-start = ((f32[16,1,6912]{2,1,0:T(1,128)}), f32[16,1,6912]{2,1,0:T(1,128)S(1)}, u32[]{:S(2)}, u32[]{:S(2)}) async-start(f32[16,1,6912]{2,1,0:T(1,128)} %reshape.200), calls=%async_computation | async-start | bytes 884736 | tf_op jit(solution)/shard_map/all_to_all | solution.py:42
  35.3 29.2 %all-to-all-start.1 = ((f32[32,1,576]{2,1,0:T(1,128)}), f32[32,1,576]{2,1,0:T(1,128)S(1)}, u32[]{:S(2)}, u32[]{:S(2)}) async-start(f32[32,1,576]{2,1,0:T(1,128)} %reshape.201), calls=%async_computation.1 | async-start | bytes 163840 | tf_op jit(solution)/shard_map/all_to_all | solution.py:61
  64.8 20.4 %copy-start = (f32[384,384]{1,0:T(8,128)S(1)}, f32[384,384]{1,0:T(8,128)}, u32[]{:S(2)}) copy-start(f32[384,384]{1,0:T(8,128)} %constant.60.clone) | copy-start | bytes 1769476
  109.7 2.7 %copy-start.2 = (f32[384,384,1]{1,0,2:T(8,128)S(1)}, f32[384,384,1]{1,0,2:T(8,128)}, u32[]{:S(2)}) copy-start(f32[384,384,1]{1,0,2:T(8,128)} %constant.69) | copy-start | bytes 1769476
where the time goes:
time: 114 us
  blocking collectives  33.5 us (29%)
  starting transfers between devices  26.7 us (23%)
  waiting for transfers between devices  26 us (23%)
  local copies, waits for them, and re-layouts  16.1 us (14%)
  matrix products  6.4 us (6%)
  other arithmetic  4.79 us (4%)
    all_to_all x1, blocking collectives, body(): lax.all_to_all(chunks.reshape(n_row, 1, per), 'row', 0, 0, tiled=True)  18.4 us
    all_to_all x1, blocking collectives, body(): lax.all_to_all(lines.reshape(group, 1, na * nb * ns), ('rep', 'col'), 0,...  15.1 us
    all_to_all x1, waiting for transfers between devices, body(): waves = lax.all_to_all(waves, 'row', 0, 0, tiled=True)  15 us
    all_to_all x1, starting transfers between devices, body(): waves = lax.all_to_all(waves, 'row', 0, 0, tiled=True)  14 us
    all_to_all x1, waiting for transfers between devices, body(): lax.all_to_all(modes.reshape(group, 1, na * nb * ns), ('rep', 'col'), 0,...  9.6 us
    ppermute x1, starting transfers between devices, body(): density = mine + lax.ppermute(other, 'rep', [(0, 1), (1, 0)])  8.75 us
    dot_general x4, matrix products, dot3(): lax.dot_general(a, b, (dims, ((), ())), precision=lax.Precision.HIGH, pre...  6.4 us
    all_to_all x1, starting transfers between devices, body(): lax.all_to_all(modes.reshape(group, 1, na * nb * ns), ('rep', 'col'), 0,...  3.9 us
  transfers between devices with their start and end apart: 3, of which 3 were waited for; matrix products, arithmetic and copies ran while one was open for 0% of the time, Pallas kernels for 0%

commit v1 on v0

v1 whole, which is shorter than its diff:
```python
import ml_dtypes
import numpy as np

import jax
import jax.numpy as jnp
from jax import lax
from jax.experimental import pallas as pl
from jax.experimental.pallas import tpu as pltpu
from jax.sharding import PartitionSpec as P

N = 384
SHIFT = 0.001
REP, COL, ROW = 2, 8, 32
GROUP = REP * COL
BLOCK = N // GROUP
CELLS = N // ROW
LINES = CELLS * BLOCK
TILES = BLOCK // 8
PACKED = 2 * TILES + 1
F32 = jnp.float32
BF16 = jnp.bfloat16


def block_of(member):
    return member % COL * REP + member // COL


def member_of(block):
    return block % REP * COL + block // REP


def tables():
    order = [
        BLOCK * block_of(member) + 8 * tile + low
        for tile in range(TILES)
        for member in range(GROUP)
        for low in range(8)
    ]
    turns = np.outer(np.asarray(order), np.arange(N)) % N
    angle = turns * (2.0 * np.pi / N)
    cas = np.cos(angle) + np.sin(angle)
    high = cas.astype(ml_dtypes.bfloat16)
    low = (cas - high.astype(np.float64)).astype(ml_dtypes.bfloat16)
    return high, low


def eigen_line():
    return (4.0 * np.sin(np.pi * np.arange(N) / N) ** 2).astype(np.float32)


def halves(x):
    high = x.astype(BF16)
    return high, (x - high.astype(F32)).astype(BF16)


def product(first, second, contract):
    dims = (contract, ((), ()))
    (fh, fl), (sh, sl) = first, second
    out = lax.dot_general(fl, sh, dims, preferred_element_type=F32)
    out += lax.dot_general(fh, sl, dims, preferred_element_type=F32)
    return out + lax.dot_general(fh, sh, dims, preferred_element_type=F32)


def lanes(shape):
    return lax.broadcasted_iota(jnp.int32, shape, 1)


def swapped(parts, width):
    parts = list(parts)
    lane = lanes(parts[0].shape)
    bit = 1
    while bit < len(parts):
        reach = width * bit
        upper = (lane & reach) != 0
        for i in range(len(parts)):
            if i & bit:
                continue
            a, b = parts[i], parts[i | bit]
            parts[i] = jnp.where(upper, pltpu.roll(b, reach, 1), a)
            parts[i | bit] = jnp.where(upper, b, pltpu.roll(a, 128 - reach, 1))
        bit *= 2
    return parts


def send_lines(lines, high_ref, low_ref, out_ref, slot_of):
    pad = jnp.zeros((N - LINES, N), BF16)
    lines = tuple(jnp.concatenate([part, pad], 0) for part in halves(lines))
    got = product((high_ref[...], low_ref[...]), lines, ((1,), (1,)))
    rows = 8 * GROUP
    lane = lanes((rows, 128))
    rest = got[0:rows, 256:384]
    for tile in range(1, TILES):
        moved = pltpu.roll(got[rows * tile : rows * (tile + 1), 256:384], 32 * tile, 1)
        rest = jnp.where(lane < 32 * tile, rest, moved)
    for member in range(GROUP):
        slot = slot_of(member)
        for tile in range(TILES):
            at = rows * tile + 8 * member
            for half in range(2):
                to = 8 * (2 * tile + half)
                out_ref[slot, to : to + 8, :] = got[at : at + 8, 128 * half : 128 * half + 128]
        to = 8 * (PACKED - 1)
        out_ref[slot, to : to + 8, :] = rest[8 * member : 8 * member + 8]


def received_lines(in_ref, lines_ref):
    parts = swapped([in_ref[member] for member in range(GROUP)], 8)
    for unit in range(CELLS * TILES):
        cell, piece = unit // TILES, unit % TILES
        for tile in range(TILES):
            if unit < 32:
                source = parts[unit % 16]
                at = 8 * (2 * tile + unit // 16)
            else:
                source = parts[4 * tile + unit - 32]
                at = 8 * (PACKED - 1)
            to = BLOCK * cell + 8 * tile
            lines_ref[to : to + 8, 128 * piece : 128 * piece + 128] = source[at : at + 8]


def ratio_of(lam):
    root = jnp.sqrt(lam * (lam + 4.0))
    return 2.0 / (2.0 + lam + root), root


def pieces_of(x):
    return [
        x[8 * tile : 8 * tile + 8, 128 * part : 128 * part + 128]
        for tile in range(TILES)
        for part in range(N // 128)
    ]


def first_kernel(mine_ref, got_ref, high_ref, low_ref, out_ref):
    density = (mine_ref[...] + got_ref[...]).reshape(LINES, N)
    send_lines(density, high_ref, low_ref, out_ref, lambda member: member)


def second_kernel(in_ref, lam_ref, high_ref, low_ref, field_ref, waves_ref, step_ref, lines_ref):
    received_lines(in_ref, lines_ref)
    table = (high_ref[...], low_ref[...])
    field_ref[...] = product(halves(lines_ref[...]), table, ((1,), (0,)))
    ratio, _ = ratio_of(lam_ref[...])
    right = field_ref[0:BLOCK, :]
    left = field_ref[LINES - BLOCK : LINES, :]
    for i in range(1, CELLS):
        right = right * ratio + field_ref[BLOCK * i : BLOCK * (i + 1), :]
        j = CELLS - 1 - i
        left = left * ratio + field_ref[BLOCK * j : BLOCK * (j + 1), :]
    square = ratio * ratio
    fourth = square * square
    step = pieces_of(fourth * fourth * fourth)
    right, left = pieces_of(right), pieces_of(left)
    empty = jnp.zeros((8, 128), F32)
    extra = (right[8], left[8], empty, empty)
    parts = swapped(
        [
            jnp.concatenate([right[k], right[4 + k], left[k], left[4 + k], extra[k]], 0)
            for k in range(4)
        ],
        32,
    )
    for quarter in range(4):
        for m in range(5):
            row = parts[quarter][8 * m : 8 * m + 8].reshape(8, 1, 128)
            waves_ref[8 * quarter : 8 * quarter + 8, :, 128 * m : 128 * m + 128] = row
    extra = (step[8], step[8], empty, empty)
    parts = swapped([jnp.concatenate([step[k], step[4 + k], extra[k]], 0) for k in range(4)], 32)
    for quarter in range(4):
        for m in range(3):
            to = 8 * (4 * m + quarter)
            step_ref[to : to + 8, :] = parts[quarter][8 * m : 8 * m + 8]


def ring_kernel(row_ref, in_ref, step_ref, out_ref):
    row = row_ref[0]
    low_lane = lanes((ROW, 128)) < 32
    for m in range(5):
        lane_tile = (0, 1, 0, 1, 2)[m]
        step = step_ref[pl.ds(ROW * lane_tile + row, 1), :]
        chunks = in_ref[:, :, 128 * m : 128 * m + 128].reshape(ROW, 128)

        def moved(x, reach):
            if m < 2:
                return pltpu.roll(x, reach, 0)
            if m < 4:
                return pltpu.roll(x, ROW - reach, 0)
            return jnp.where(low_lane, pltpu.roll(x, reach, 0), pltpu.roll(x, ROW - reach, 0))

        reach = 1
        while reach < ROW:
            chunks = chunks + step * moved(chunks, reach)
            step = step * step
            reach *= 2
        chunks = moved(chunks / (1.0 - step), 1)
        out_ref[:, :, 128 * m : 128 * m + 128] = chunks.reshape(ROW, 1, 128)


def third_kernel(field_ref, in_ref, lam_ref, high_ref, low_ref, out_ref, lines_ref):
    parts = swapped(
        [
            jnp.concatenate(
                [
                    in_ref[8 * quarter : 8 * quarter + 8, :, 128 * m : 128 * m + 128].reshape(8, 128)
                    for m in range(5)
                ],
                0,
            )
            for quarter in range(4)
        ],
        32,
    )

    def joined(first, second, last):
        tiles = [parts[k][8 * first : 8 * first + 8] for k in range(4)]
        tiles += [parts[k][8 * second : 8 * second + 8] for k in range(4)]
        tiles.append(parts[last][32:40])
        return jnp.concatenate([jnp.concatenate(tiles[3 * t : 3 * t + 3], 1) for t in range(3)], 0)

    ratio, root = ratio_of(lam_ref[...])
    scale = (1.0 / (N * N)) / root
    run = joined(0, 1, 0)
    for i in range(CELLS):
        run = run * ratio
        lines_ref[BLOCK * i : BLOCK * (i + 1), :] = run
        run = run + field_ref[BLOCK * i : BLOCK * (i + 1), :]
    run = joined(2, 3, 1)
    for i in range(CELLS - 1, -1, -1):
        at = slice(BLOCK * i, BLOCK * (i + 1))
        run = run * ratio + field_ref[at, :]
        lines_ref[at, :] = (lines_ref[at, :] + run) * scale
    send_lines(lines_ref[...], high_ref, low_ref, out_ref, block_of)


def last_kernel(in_ref, high_ref, low_ref, out_ref, lines_ref):
    received_lines(in_ref, lines_ref)
    table = (high_ref[...], low_ref[...])
    result = product(halves(lines_ref[...]), table, ((1,), (0,)))
    out_ref[...] = result.reshape(CELLS, BLOCK, N)


def shaped(*shape):
    return jax.ShapeDtypeStruct(shape, F32)


def lines_scratch():
    return pltpu.VMEM((LINES, N), F32)


def exchange(x):
    return lax.all_to_all(x, ("rep", "col"), 0, 0, tiled=True)


def body(sources):
    rep, col, row = lax.axis_index("rep"), lax.axis_index("col"), lax.axis_index("row")
    high, low = (jnp.asarray(part) for part in tables())
    part = jnp.transpose(sources[0], (1, 0, 2))
    mine = lax.dynamic_slice_in_dim(part, rep * BLOCK, BLOCK, 1)
    other = lax.dynamic_slice_in_dim(part, (1 - rep) * BLOCK, BLOCK, 1)
    got = lax.ppermute(other, "rep", [(0, 1), (1, 0)])
    eigen = jnp.asarray(eigen_line())
    third = lax.dynamic_slice_in_dim(eigen, (col * REP + rep) * BLOCK, BLOCK)
    lam = third[:, None] + eigen[None, :] + SHIFT
    packed = shaped(GROUP, 8 * PACKED, 128)
    waves = shaped(ROW, 1, 640)
    modes = pl.pallas_call(first_kernel, out_shape=packed, name="first")(mine, got, high, low)
    field, sums, step = pl.pallas_call(
        second_kernel,
        out_shape=(shaped(LINES, N), waves, shaped(3 * ROW, 128)),
        scratch_shapes=[lines_scratch()],
        name="second",
    )(exchange(modes), lam, high, low)
    sums = lax.all_to_all(sums, "row", 0, 0, tiled=True)
    vmem = pl.BlockSpec(memory_space=pltpu.VMEM)
    sums = pl.pallas_call(
        ring_kernel,
        in_specs=[pl.BlockSpec(memory_space=pltpu.SMEM), vmem, vmem],
        out_shape=waves,
        name="ring",
    )(row.reshape(1), sums, step)
    sums = lax.all_to_all(sums, "row", 0, 0, tiled=True)
    lines = pl.pallas_call(
        third_kernel, out_shape=packed, scratch_shapes=[lines_scratch()], name="third"
    )(field, sums, lam, high, low)
    result = pl.pallas_call(
        last_kernel,
        out_shape=shaped(CELLS, BLOCK, N),
        scratch_shapes=[lines_scratch()],
        name="last",
    )(exchange(lines), high, low)
    return jnp.transpose(result, (1, 0, 2))


def solution(mesh):
    return jax.shard_map(
        body,
        mesh=mesh,
        in_specs=(P("rep", "col", "row", None),),
        out_specs=P(("rep", "col"), "row", None),
        check_vma=False,
    )
```

time: 114 us -> 108 us (0.947)
  Pallas kernels: 0 us -> 13.6 us
  local copies, waits for them, and re-layouts: 16.1 us -> 4.87 us
  matrix products: 6.4 us -> 0 us
  other arithmetic: 4.79 us -> 0.68 us
  blocking collectives: 33.5 us -> 36.9 us
    pallas_call x0 -> x5, Pallas kernels: none -> 13.6 us  [the longest x1 3.09 us: body(): pl.pallas_call(second_kernel, out_shape=(shaped(LINES, N), waves, shaped(...]
    reshape x6 -> x0, local copies, waits for them, and re-layouts: 7.35 us -> none  [the longest x1 2.71 us: body(): lines.reshape(group, na, nb, ns).transpose(1, 2, 0, 3).reshape(na * nb, N)]
    dot_general x4 -> x0, matrix products: 6.4 us -> none  [dot3(): lax.dot_general(a, b, (dims, ((), ())), precision=lax.Precision.HIGH, pre...]
    transpose x2 -> x0, local copies, waits for them, and re-layouts: 4.22 us -> none  [the longest x1 2.8 us: body(): lines.reshape(group, na, nb, ns).transpose(1, 2, 0, 3).reshape(na * nb, N)]
    all_to_all x2, blocking collectives: 33.5 us -> 36.9 us  [the longest x1 19.6 us: body(): sums = lax.all_to_all(sums, 'row', 0, 0, tiled=True)]
    all_to_all x2 -> x0, other arithmetic: 2.93 us -> none  [the longest x1 1.88 us: body(): lax.all_to_all(lines.reshape(group, 1, na * nb * ns), ('rep', 'col'), 0,...]
    unnamed x8, local copies, waits for them, and re-layouts: 0.02 us -> 2.83 us
    dot_general x1 -> x0, local copies, waits for them, and re-layouts: 2.67 us -> none  [dot3(): lax.dot_general(a, b, (dims, ((), ())), precision=lax.Precision.HIGH, pre...]
  transfers between devices with their start and end apart: 3 -> 3, of which waited for: 3 -> 3; matrix products, arithmetic and copies ran while one was open for 0% -> 1% of each run, Pallas kernels for 0% -> 0%
where the time goes in v1:
time: 108 us
  blocking collectives  36.9 us (34%)
  starting transfers between devices  26.5 us (25%)
  waiting for transfers between devices  25 us (23%)
  Pallas kernels  13.6 us (13%)
  local copies, waits for them, and re-layouts  4.87 us (5%)
    all_to_all x1, blocking collectives, body(): sums = lax.all_to_all(sums, 'row', 0, 0, tiled=True)  19.6 us
    all_to_all x1, blocking collectives, exchange(): return lax.all_to_all(x, ('rep', 'col'), 0, 0, tiled=True)  17.3 us
    all_to_all x1, waiting for transfers between devices, body(): sums = lax.all_to_all(sums, 'row', 0, 0, tiled=True)  15.1 us
    all_to_all x1, starting transfers between devices, body(): sums = lax.all_to_all(sums, 'row', 0, 0, tiled=True)  14 us
    ppermute x1, starting transfers between devices, body(): got = lax.ppermute(other, 'rep', [(0, 1), (1, 0)])  8.73 us
    all_to_all x1, waiting for transfers between devices, exchange(): return lax.all_to_all(x, ('rep', 'col'), 0, 0, tiled=True)  8.42 us
    all_to_all x1, starting transfers between devices, exchange(): return lax.all_to_all(x, ('rep', 'col'), 0, 0, tiled=True)  3.77 us
    pallas_call x1, Pallas kernels, body(): pl.pallas_call(second_kernel, out_shape=(shaped(LINES, N), waves, shaped(...  3.09 us
  transfers between devices with their start and end apart: 3, of which 3 were waited for; matrix products, arithmetic and copies ran while one was open for 1% of the time, Pallas kernels for 0%

profile of v1, /device:TPU:1, one launch (start us, length us, event | category | flops | bytes accessed | tf_op | source)
XLA Modules:
  0.0 107.5 jit_solution(13496256620756622428)
XLA Ops:
  0.0 2.0 %dynamic-slice_bitcast_fusion = (f32[12,24,384]{2,1,0:T(8,128)S(1)}, f32[12,24,384]{2,1,0:T(8,128)}) fusion(f32[1,48,12,384]{3,1,2,0:T(8,128)} %param.4, s32[]{:T(128)S(6)} %select_n.10, s32[]{:T(128)S(6)} %select_n.9), kind=kLoop, calls=%fused_computation | loop fusion | bytes 1769480 | tf_op jit(solution)/shard_map/dynamic_slice | solution.py:259
  2.0 8.7 %collective-permute-start = (f32[12,24,384]{2,1,0:T(8,128)S(1)}, f32[12,24,384]{2,1,0:T(8,128)S(1)}, u32[]{:S(2)}, u32[]{:S(2)}) collective-permute-start(f32[12,24,384]{2,1,0:T(8,128)S(1)} %get-tuple-element.11), channel_id=1, source_target_pairs={{0,256},{256,0},{1,257},{257,1},{2,258},{258,2},{3,259},{259,3},{4... | collective-permute-start | bytes 1327112 | tf_op jit(solution)/shard_map/ppermute | solution.py:260
  10.7 1.4 %collective-permute-done.got_ref = f32[12,24,384]{2,1,0:T(8,128)S(1)} collective-permute-done((f32[12,24,384]{2,1,0:T(8,128)S(1)}, f32[12,24,384]{2,1,0:T(8,128)S(1)}, u32[]{:S(2)}, u32[]{:S(2)}) %collective-permute-start) | collective-permute-done | bytes 442400 | tf_op jit(solution)/shard_map/ppermute | solution.py:260
  12.1 0.0 copy-start.1
  12.1 0.8 copy-done.1
  12.9 2.9 %first.1 = f32[16,56,128]{2,1,0:T(8,128)} custom-call(f32[12,24,384]{2,1,0:T(8,128)} %get-tuple-element.12.mine_ref, f32[12,24,384]{2,1,0:T(8,128)} %copy-done.1, bf16[384,384]{1,0:T(8,128)(2,1)} %constant.37.clone.high_ref, bf16[384,384]{1,0:T(8,128)(2,1)} %constant.38.clone.low_ref), custom_call_target="tpu_custom_call" | custom-call | tf_op jit(solution)/shard_map/first/pallas_call | solution.py:266
  15.7 3.8 %all-to-all-start = ((f32[16,56,128]{2,1,0:T(8,128)}), f32[16,56,128]{2,1,0:T(8,128)S(1)}, u32[]{:S(2)}, u32[]{:S(2)}) async-start(f32[16,56,128]{2,1,0:T(8,128)} %first.1), calls=%async_computation | async-start | bytes 917504 | tf_op jit(solution)/shard_map/all_to_all | solution.py:251
  19.5 0.0 copy-start.3
  19.5 0.7 copy-done.3
  20.2 0.1 dynamic_slice.11
  20.3 0.7 add_add_fusion.lam_ref
  20.9 8.4 %all-to-all-done.in_ref = f32[16,56,128]{2,1,0:T(8,128)S(1)} async-done(((f32[16,56,128]{2,1,0:T(8,128)}), f32[16,56,128]{2,1,0:T(8,128)S(1)}, u32[]{:S(2)}, u32[]{:S(2)}) %all-to-all-start) | async-done | bytes 458784 | tf_op jit(solution)/shard_map/all_to_all | solution.py:251
  29.4 0.0 copy-start
  29.4 0.8 copy-done
  30.1 3.1 %second.1 = (f32[288,384]{1,0:T(8,128)}, f32[32,1,640]{2,1,0:T(1,128)}, f32[96,128]{1,0:T(8,128)}) custom-call(f32[16,56,128]{2,1,0:T(8,128)} %copy-done, f32[24,384]{1,0:T(8,128)} %add_add_fusion.lam_ref, bf16[384,384]{1,0:T(8,128)(2,1)} %constant.37.clone.high_ref, bf16[384,384]{1,0:T(8,128)(2,1)} %constant.38.clone.low_ref), custom_call_target="tpu_custom_call" | custom-call | tf_op jit(solution)/shard_map/second/pallas_call | solution.py:267
  33.2 14.0 %all-to-all-start.1 = ((f32[32,1,640]{2,1,0:T(1,128)}), f32[32,1,640]{2,1,0:T(1,128)S(1)}, u32[]{:S(2)}, u32[]{:S(2)}) async-start(f32[32,1,640]{2,1,0:T(1,128)} %get-tuple-element.9), calls=%async_computation.1 | async-start | bytes 163840 | tf_op jit(solution)/shard_map/all_to_all | solution.py:273
  47.2 15.1 %all-to-all-done.1.in_ref = f32[32,1,640]{2,1,0:T(1,128)S(1)} async-done(((f32[32,1,640]{2,1,0:T(1,128)}), f32[32,1,640]{2,1,0:T(1,128)S(1)}, u32[]{:S(2)}, u32[]{:S(2)}) %all-to-all-start.1) | async-done | bytes 81952 | tf_op jit(solution)/shard_map/all_to_all | solution.py:273
  62.4 0.0 copy-start.2
  62.4 0.6 copy-done.2
  63.0 1.7 %ring.1 = f32[32,1,640]{2,1,0:T(1,128)} custom-call(s32[1]{0:T(128)} %bitcast.4.row_ref, f32[32,1,640]{2,1,0:T(1,128)} %copy-done.2, f32[96,128]{1,0:T(8,128)} %get-tuple-element.10.step_ref), custom_call_target="tpu_custom_call" | custom-call | tf_op jit(solution)/shard_map/ring/pallas_call | solution.py:275
  64.7 19.6 %all_to_all.20.in_ref = f32[32,1,640]{2,1,0:T(1,128)} all-to-all(f32[32,1,640]{2,1,0:T(1,128)} %ring.1), channel_id=1, replica_groups=mesh['rep'=2,'row'=32,'col'=8] {'row'}, dimensions={0} | all-to-all | bytes 163840 | tf_op jit(solution)/shard_map/all_to_all | solution.py:281
  84.2 3.0 %third.1 = f32[16,56,128]{2,1,0:T(8,128)} custom-call(f32[288,384]{1,0:T(8,128)} %get-tuple-element.8.field_ref, f32[32,1,640]{2,1,0:T(1,128)} %all_to_all.20.in_ref, f32[24,384]{1,0:T(8,128)} %add_add_fusion.lam_ref, bf16[384,384]{1,0:T(8,128)(2,1)} %constant.37.clone.high_ref, bf16[384,384]{1,0:T(8,128)(2,1)} %constant.38.clone.low_ref), custom_call_target="tpu_custom_call" | custom-call | tf_op jit(solution)/shard_map/third/pallas_call | solution.py:282
  87.2 17.3 %all_to_all.21.in_ref = f32[16,56,128]{2,1,0:T(8,128)} all-to-all(f32[16,56,128]{2,1,0:T(8,128)} %third.1), channel_id=1, replica_groups=mesh['rep'=2,'row'=32,'col'=8] {'rep','col'}, dimensions={0} | all-to-all | bytes 917504 | tf_op jit(solution)/shard_map/all_to_all | solution.py:251
  104.5 3.0 %last.1 = f32[12,24,384]{2,1,0:T(8,128)} custom-call(f32[16,56,128]{2,1,0:T(8,128)} %all_to_all.21.in_ref, bf16[384,384]{1,0:T(8,128)(2,1)} %constant.37.clone.high_ref, bf16[384,384]{1,0:T(8,128)(2,1)} %constant.38.clone.low_ref), custom_call_target="tpu_custom_call" | custom-call | tf_op jit(solution)/shard_map/last/pallas_call | solution.py:285
Async XLA Ops:
  2.0 10.1 %collective-permute-start = (f32[12,24,384]{2,1,0:T(8,128)S(1)}, f32[12,24,384]{2,1,0:T(8,128)S(1)}, u32[]{:S(2)}, u32[]{:S(2)}) collective-permute-start(f32[12,24,384]{2,1,0:T(8,128)S(1)} %get-tuple-element.11), channel_id=1, source_target_pairs={{0,256},{256,0},{1,257},{257,1},{2,258},{258,2},{3,259},{259,3},{4... | collective-permute-start | bytes 1327112 | tf_op jit(solution)/shard_map/ppermute | solution.py:260
  12.1 0.8 copy-start.1
  15.7 13.6 %all-to-all-start = ((f32[16,56,128]{2,1,0:T(8,128)}), f32[16,56,128]{2,1,0:T(8,128)S(1)}, u32[]{:S(2)}, u32[]{:S(2)}) async-start(f32[16,56,128]{2,1,0:T(8,128)} %first.1), calls=%async_computation | async-start | bytes 917504 | tf_op jit(solution)/shard_map/all_to_all | solution.py:251
  19.5 0.7 copy-start.3
  29.4 0.8 copy-start
  33.2 29.1 %all-to-all-start.1 = ((f32[32,1,640]{2,1,0:T(1,128)}), f32[32,1,640]{2,1,0:T(1,128)S(1)}, u32[]{:S(2)}, u32[]{:S(2)}) async-start(f32[32,1,640]{2,1,0:T(1,128)} %get-tuple-element.9), calls=%async_computation.1 | async-start | bytes 163840 | tf_op jit(solution)/shard_map/all_to_all | solution.py:273
  62.4 0.6 copy-start.2

commit v2 on v1

--- a/solution.py
+++ b/solution.py
@@ -17,6 +17,7 @@
 LINES = CELLS * BLOCK
 TILES = BLOCK // 8
 PACKED = 2 * TILES + 1
+VMEM_BYTES = 12 * 2**20
 F32 = jnp.float32
 BF16 = jnp.bfloat16
 
@@ -239,12 +240,33 @@
     out_ref[...] = result.reshape(CELLS, BLOCK, N)
 
 
+def call(kernel, name, **kwargs):
+    params = pltpu.CompilerParams(vmem_limit_bytes=VMEM_BYTES)
+    return pl.pallas_call(kernel, name=name, compiler_params=params, **kwargs)
+
+
 def shaped(*shape):
     return jax.ShapeDtypeStruct(shape, F32)
 
 
 def lines_scratch():
     return pltpu.VMEM((LINES, N), F32)
+
+
+def copy_kernel(rep_ref, in_ref, out_ref):
+    out_ref[...] = in_ref[...]
+
+
+def own_half(part, rep):
+    shape = (CELLS, BLOCK, N)
+    grid_spec = pltpu.PrefetchScalarGridSpec(
+        num_scalar_prefetch=1,
+        grid=(1,),
+        in_specs=[pl.BlockSpec(shape, lambda i, rep_ref: (0, rep_ref[0], 0))],
+        out_specs=pl.BlockSpec(shape, lambda i, rep_ref: (0, 0, 0)),
+    )
+    out = shaped(*shape)
+    return call(copy_kernel, "mine", grid_spec=grid_spec, out_shape=out)(rep.reshape(1), part)
 
 
 def exchange(x):
@@ -255,7 +277,7 @@
     rep, col, row = lax.axis_index("rep"), lax.axis_index("col"), lax.axis_index("row")
     high, low = (jnp.asarray(part) for part in tables())
     part = jnp.transpose(sources[0], (1, 0, 2))
-    mine = lax.dynamic_slice_in_dim(part, rep * BLOCK, BLOCK, 1)
+    mine = own_half(part, rep)
     other = lax.dynamic_slice_in_dim(part, (1 - rep) * BLOCK, BLOCK, 1)
     got = lax.ppermute(other, "rep", [(0, 1), (1, 0)])
     eigen = jnp.asarray(eigen_line())
@@ -263,30 +285,31 @@
     lam = third[:, None] + eigen[None, :] + SHIFT
     packed = shaped(GROUP, 8 * PACKED, 128)
     waves = shaped(ROW, 1, 640)
-    modes = pl.pallas_call(first_kernel, out_shape=packed, name="first")(mine, got, high, low)
-    field, sums, step = pl.pallas_call(
+    modes = call(first_kernel, "first", out_shape=packed)(mine, got, high, low)
+    modes, lam, place = lax.optimization_barrier((modes, lam, row.reshape(1)))
+    field, sums, step = call(
         second_kernel,
+        "second",
         out_shape=(shaped(LINES, N), waves, shaped(3 * ROW, 128)),
         scratch_shapes=[lines_scratch()],
-        name="second",
     )(exchange(modes), lam, high, low)
     sums = lax.all_to_all(sums, "row", 0, 0, tiled=True)
     vmem = pl.BlockSpec(memory_space=pltpu.VMEM)
-    sums = pl.pallas_call(
+    sums = call(
         ring_kernel,
+        "ring",
         in_specs=[pl.BlockSpec(memory_space=pltpu.SMEM), vmem, vmem],
         out_shape=waves,
-        name="ring",
-    )(row.reshape(1), sums, step)
+    )(place, sums, step)
     sums = lax.all_to_all(sums, "row", 0, 0, tiled=True)
-    lines = pl.pallas_call(
-        third_kernel, out_shape=packed, scratch_shapes=[lines_scratch()], name="third"
-    )(field, sums, lam, high, low)
-    result = pl.pallas_call(
+    lines = call(third_kernel, "third", out_shape=packed, scratch_shapes=[lines_scratch()])(
+        field, sums, lam, high, low
+    )
+    result = call(
         last_kernel,
+        "last",
         out_shape=shaped(CELLS, BLOCK, N),
         scratch_shapes=[lines_scratch()],
-        name="last",
     )(exchange(lines), high, low)
     return jnp.transpose(result, (1, 0, 2))
 

time: 108 us -> 92.6 us (0.86)
  blocking collectives: 36.9 us -> 76.1 us
  waiting for transfers between devices: 25 us -> 0.54 us
  starting transfers between devices: 26.5 us -> 8.75 us
  Pallas kernels: 13.6 us -> 4.94 us
  local copies, waits for them, and re-layouts: 4.87 us -> 1.83 us
    all_to_all x1 -> x2, blocking collectives: 19.6 us -> 48.2 us  [body(): sums = lax.all_to_all(sums, 'row', 0, 0, tiled=True)]
    all_to_all x2 -> x0, waiting for transfers between devices: 23.6 us -> none  [the longest x1 15.1 us: body(): sums = lax.all_to_all(sums, 'row', 0, 0, tiled=True)]
    all_to_all x2 -> x0, starting transfers between devices: 17.8 us -> none  [the longest x1 14 us: body(): sums = lax.all_to_all(sums, 'row', 0, 0, tiled=True)]
    all_to_all x1 -> x2, blocking collectives: 17.3 us -> 27.9 us  [exchange(): return lax.all_to_all(x, ('rep', 'col'), 0, 0, tiled=True)]
    pallas_call x5 -> x6, Pallas kernels: 13.6 us -> 4.94 us  [the longest x1 1.77 us: body(): call(last_kernel, 'last', out_shape=shaped(CELLS, BLOCK, N), scratch_shap...]
    unnamed x8, local copies, waits for them, and re-layouts: 2.83 us -> 0.63 us
  transfers between devices with their start and end apart: 3 -> 1, of which waited for: 3 -> 1; matrix products, arithmetic and copies ran while one was open for 1% -> 0% of each run, Pallas kernels for 0% -> 0%
where the time goes in v2:
time: 92.6 us; the launch traced here: 92.3 us
  blocking collectives  76.1 us (82%)
  starting transfers between devices  8.75 us (9%)
  Pallas kernels  4.94 us (5%)
  local copies, waits for them, and re-layouts  1.83 us (2%)
    all_to_all x2, blocking collectives, body(): sums = lax.all_to_all(sums, 'row', 0, 0, tiled=True)  48.2 us
    all_to_all x2, blocking collectives, exchange(): return lax.all_to_all(x, ('rep', 'col'), 0, 0, tiled=True)  27.9 us
    ppermute x1, starting transfers between devices, body(): got = lax.ppermute(other, 'rep', [(0, 1), (1, 0)])  8.75 us
  transfers between devices with their start and end apart: 1, of which 1 were waited for; matrix products, arithmetic and copies ran while one was open for 0% of the time, Pallas kernels for 0%

profile of v2, /device:TPU:1, one launch (start us, length us, event | category | flops | bytes accessed | tf_op | source)
XLA Modules:
  0.0 92.3 jit_solution(16215194608467834798)
XLA Ops:
  0.0 0.0 copy-start.2
  0.0 1.1 %dynamic-slice_bitcast_fusion = f32[12,24,384]{2,1,0:T(8,128)S(1)} fusion(f32[1,48,12,384]{3,1,2,0:T(8,128)} %param.4, s32[]{:T(128)S(6)} %select_n.6), kind=kLoop, calls=%fused_computation | loop fusion | bytes 884740 | tf_op jit(solution)/shard_map/dynamic_slice | solution.py:281
  1.1 8.7 %collective-permute-start = (f32[12,24,384]{2,1,0:T(8,128)S(1)}, f32[12,24,384]{2,1,0:T(8,128)S(1)}, u32[]{:S(2)}, u32[]{:S(2)}) collective-permute-start(f32[12,24,384]{2,1,0:T(8,128)S(1)} %dynamic-slice_bitcast_fusion), channel_id=1, source_target_pairs={{0,256},{256,0},{1,257},{257,1},{2,258},{258,2},{3,259},{259,3},{4... | collective-permute-start | bytes 1327112 | tf_op jit(solution)/shard_map/ppermute | solution.py:282
  9.9 0.0 copy-done.2
  9.9 0.0 copy-start.3
  9.9 0.0 copy-start
  9.9 0.0 copy-start.1
  10.0 0.6 copy-done.3
  10.6 0.1 dynamic_slice.7
  10.7 0.1 add_add_fusion.lam_ref
  10.7 0.5 collective-permute-done.got_ref
  11.3 0.0 copy-done
  11.3 0.0 copy-done.1
  11.3 0.8 first.1
  12.1 12.7 %all_to_all.20.in_ref = f32[16,56,128]{2,1,0:T(8,128)S(1)} all-to-all(f32[16,56,128]{2,1,0:T(8,128)S(1)} %first.1), channel_id=1, replica_groups=mesh['rep'=2,'row'=32,'col'=8] {'rep','col'}, dimensions={0} | all-to-all | bytes 917504 | tf_op jit(solution)/shard_map/all_to_all | solution.py:273
  24.8 1.2 %second.1 = (f32[288,384]{1,0:T(8,128)S(1)}, f32[32,1,640]{2,1,0:T(1,128)S(1)}, f32[96,128]{1,0:T(8,128)S(1)}) custom-call(f32[16,56,128]{2,1,0:T(8,128)S(1)} %all_to_all.20.in_ref, f32[24,384]{1,0:T(8,128)S(1)} %add_add_fusion.lam_ref, bf16[384,384]{1,0:T(8,128)(2,1)S(1)} %copy-done, bf16[384,384]{1,0:T(8,128)(2,1)S(1)} %copy-done.1), custom_call_target="tpu_custom_call" | custom-call | tf_op jit(solution)/shard_map/second/pallas_call | solution.py:290
  26.0 29.7 %all_to_all.21.in_ref = f32[32,1,640]{2,1,0:T(1,128)S(1)} all-to-all(f32[32,1,640]{2,1,0:T(1,128)S(1)} %get-tuple-element.15), channel_id=1, replica_groups=mesh['rep'=2,'row'=32,'col'=8] {'row'}, dimensions={0} | all-to-all | bytes 163840 | tf_op jit(solution)/shard_map/all_to_all | solution.py:296
  55.7 0.1 ring.1
  55.8 18.5 %all_to_all.22.in_ref = f32[32,1,640]{2,1,0:T(1,128)S(1)} all-to-all(f32[32,1,640]{2,1,0:T(1,128)S(1)} %ring.1), channel_id=1, replica_groups=mesh['rep'=2,'row'=32,'col'=8] {'row'}, dimensions={0} | all-to-all | bytes 163840 | tf_op jit(solution)/shard_map/all_to_all | solution.py:304
  74.4 1.0 %third.1 = f32[16,56,128]{2,1,0:T(8,128)S(1)} custom-call(f32[288,384]{1,0:T(8,128)S(1)} %get-tuple-element.13.field_ref, f32[32,1,640]{2,1,0:T(1,128)S(1)} %all_to_all.22.in_ref, f32[24,384]{1,0:T(8,128)S(1)} %add_add_fusion.lam_ref, bf16[384,384]{1,0:T(8,128)(2,1)S(1)} %copy-done, bf16[384,384]{1,0:T(8,128)(2,1)S(1)} %copy-done.1), custom_call_target="tpu_custom_call" | custom-call | tf_op jit(solution)/shard_map/third/pallas_call | solution.py:305
  75.4 15.2 %all_to_all.23.in_ref = f32[16,56,128]{2,1,0:T(8,128)S(1)} all-to-all(f32[16,56,128]{2,1,0:T(8,128)S(1)} %third.1), channel_id=1, replica_groups=mesh['rep'=2,'row'=32,'col'=8] {'rep','col'}, dimensions={0} | all-to-all | bytes 917504 | tf_op jit(solution)/shard_map/all_to_all | solution.py:273
  90.5 1.8 %last.1 = f32[12,24,384]{2,1,0:T(8,128)} custom-call(f32[16,56,128]{2,1,0:T(8,128)S(1)} %all_to_all.23.in_ref, bf16[384,384]{1,0:T(8,128)(2,1)S(1)} %copy-done, bf16[384,384]{1,0:T(8,128)(2,1)S(1)} %copy-done.1), custom_call_target="tpu_custom_call" | custom-call | tf_op jit(solution)/shard_map/last/pallas_call | solution.py:308
  (1 shorter events, 0.0 us)
Async XLA Ops:
  0.0 9.9 %copy-start.2 = (f32[1,48,12,384]{3,1,2,0:T(8,128)S(1)}, f32[1,48,12,384]{3,1,2,0:T(8,128)}, u32[]{:S(2)}) copy-start(f32[1,48,12,384]{3,1,2,0:T(8,128)} %param.4) | copy-start | bytes 2654212
  1.1 10.2 %collective-permute-start = (f32[12,24,384]{2,1,0:T(8,128)S(1)}, f32[12,24,384]{2,1,0:T(8,128)S(1)}, u32[]{:S(2)}, u32[]{:S(2)}) collective-permute-start(f32[12,24,384]{2,1,0:T(8,128)S(1)} %dynamic-slice_bitcast_fusion), channel_id=1, source_target_pairs={{0,256},{256,0},{1,257},{257,1},{2,258},{258,2},{3,259},{259,3},{4... | collective-permute-start | bytes 1327112 | tf_op jit(solution)/shard_map/ppermute | solution.py:282
  9.9 0.7 copy-start.3
  9.9 1.4 %copy-start = (bf16[384,384]{1,0:T(8,128)(2,1)S(1)}, bf16[384,384]{1,0:T(8,128)(2,1)}, u32[]{:S(2)}) copy-start(bf16[384,384]{1,0:T(8,128)(2,1)} %constant.36.clone.high_ref) | copy-start | bytes 884740
  9.9 1.4 %copy-start.1 = (bf16[384,384]{1,0:T(8,128)(2,1)S(1)}, bf16[384,384]{1,0:T(8,128)(2,1)}, u32[]{:S(2)}) copy-start(bf16[384,384]{1,0:T(8,128)(2,1)} %constant.37.clone.low_ref) | copy-start | bytes 884740

commit v3 on v2

--- a/solution.py
+++ b/solution.py
@@ -11,12 +11,15 @@
 N = 384
 SHIFT = 0.001
 REP, COL, ROW = 2, 8, 32
+ARC = ROW // 2
 GROUP = REP * COL
 BLOCK = N // GROUP
 CELLS = N // ROW
 LINES = CELLS * BLOCK
 TILES = BLOCK // 8
 PACKED = 2 * TILES + 1
+WAVES = 9
+PARTS = 3
 VMEM_BYTES = 12 * 2**20
 F32 = jnp.float32
 BF16 = jnp.bfloat16
@@ -152,80 +155,109 @@
     fourth = square * square
     step = pieces_of(fourth * fourth * fourth)
     right, left = pieces_of(right), pieces_of(left)
-    empty = jnp.zeros((8, 128), F32)
-    extra = (right[8], left[8], empty, empty)
-    parts = swapped(
-        [
-            jnp.concatenate([right[k], right[4 + k], left[k], left[4 + k], extra[k]], 0)
-            for k in range(4)
-        ],
-        32,
-    )
-    for quarter in range(4):
+    sides = []
+    for k in range(2):
+        rows = [*right[k:8:2], *left[k:8:2], (right, left)[k][8]]
+        sides.append(jnp.concatenate(rows, 0))
+    for half, side in enumerate(swapped(sides, 64)):
+        for m in range(WAVES):
+            row = side[8 * m : 8 * m + 8].reshape(8, 1, 128)
+            waves_ref[8 * half : 8 * half + 8, :, 128 * m : 128 * m + 128] = row
+    sides = [jnp.concatenate([*step[k:8:2], step[8]], 0) for k in range(2)]
+    for half, side in enumerate(swapped(sides, 64)):
         for m in range(5):
-            row = parts[quarter][8 * m : 8 * m + 8].reshape(8, 1, 128)
-            waves_ref[8 * quarter : 8 * quarter + 8, :, 128 * m : 128 * m + 128] = row
-    extra = (step[8], step[8], empty, empty)
-    parts = swapped([jnp.concatenate([step[k], step[4 + k], extra[k]], 0) for k in range(4)], 32)
-    for quarter in range(4):
-        for m in range(3):
-            to = 8 * (4 * m + quarter)
-            step_ref[to : to + 8, :] = parts[quarter][8 * m : 8 * m + 8]
-
-
-def ring_kernel(row_ref, in_ref, step_ref, out_ref):
-    row = row_ref[0]
-    low_lane = lanes((ROW, 128)) < 32
-    for m in range(5):
-        lane_tile = (0, 1, 0, 1, 2)[m]
-        step = step_ref[pl.ds(ROW * lane_tile + row, 1), :]
-        chunks = in_ref[:, :, 128 * m : 128 * m + 128].reshape(ROW, 128)
-
-        def moved(x, reach):
-            if m < 2:
-                return pltpu.roll(x, reach, 0)
+            to = 8 * (2 * m + half)
+            step_ref[to : to + 8, :] = side[8 * m : 8 * m + 8]
+
+
+def wave_step(step_ref, place, m):
+    kind = 4 if m == 8 else m % 4
+    return step_ref[pl.ds(ARC * kind + place, 1), :]
+
+
+def arc_kernel(place_ref, in_ref, step_ref, sums_ref, whole_ref):
+    place = place_ref[0]
+    chunk = lax.broadcasted_iota(jnp.int32, (ARC, 128), 0)
+    is_right = lanes((ARC, 128)) < 64
+    for m in range(WAVES):
+        step = wave_step(step_ref, place, m)
+        sums = in_ref[:, :, 128 * m : 128 * m + 128].reshape(ARC, 128)
+        reach = 1
+        while reach < ARC:
+            back = jnp.where(chunk >= reach, pltpu.roll(sums, reach, 0), 0.0)
+            ahead = jnp.where(chunk < ARC - reach, pltpu.roll(sums, ARC - reach, 0), 0.0)
             if m < 4:
-                return pltpu.roll(x, ROW - reach, 0)
-            return jnp.where(low_lane, pltpu.roll(x, reach, 0), pltpu.roll(x, ROW - reach, 0))
-
-        reach = 1
-        while reach < ROW:
-            chunks = chunks + step * moved(chunks, reach)
+                moved = back
+            elif m < 8:
+                moved = ahead
+            else:
+                moved = jnp.where(is_right, back, ahead)
+            sums = sums + step * moved
             step = step * step
             reach *= 2
-        chunks = moved(chunks / (1.0 - step), 1)
-        out_ref[:, :, 128 * m : 128 * m + 128] = chunks.reshape(ROW, 1, 128)
+        sums_ref[:, 128 * m : 128 * m + 128] = sums
+        first, last = sums[0:1], sums[ARC - 1 : ARC]
+        if m < 4:
+            whole = last
+        elif m < 8:
+            whole = first
+        else:
+            whole = jnp.where(is_right[0:1], last, first)
+        whole_ref[:, 128 * m : 128 * m + 128] = whole
+
+
+def ring_kernel(place_ref, sums_ref, whole_ref, other_ref, step_ref, out_ref):
+    place = place_ref[0]
+    chunk = lax.broadcasted_iota(jnp.int32, (ARC, 128), 0)
+    is_right = lanes((ARC, 128)) < 64
+    for m in range(WAVES):
+        at = slice(128 * m, 128 * m + 128)
+        step = wave_step(step_ref, place, m)
+        sums = sums_ref[:, at]
+        back = jnp.where(chunk >= 1, pltpu.roll(sums, 1, 0), 0.0)
+        ahead = jnp.where(chunk < ARC - 1, pltpu.roll(sums, ARC - 1, 0), 0.0)
+        if m < 4:
+            moved, depth = back, chunk
+        elif m < 8:
+            moved, depth = ahead, ARC - 1 - chunk
+        else:
+            moved = jnp.where(is_right, back, ahead)
+            depth = jnp.where(is_right, chunk, ARC - 1 - chunk)
+        decay = jnp.ones((ARC, 128), F32)
+        reach = 1
+        while reach < ARC:
+            decay = jnp.where((depth & reach) != 0, decay * step, decay)
+            step = step * step
+            reach *= 2
+        inflow = (other_ref[:, at] + step * whole_ref[:, at]) / (1.0 - step * step)
+        out_ref[:, :, at] = (moved + decay * inflow).reshape(ARC, 1, 128)
 
 
 def third_kernel(field_ref, in_ref, lam_ref, high_ref, low_ref, out_ref, lines_ref):
-    parts = swapped(
-        [
-            jnp.concatenate(
-                [
-                    in_ref[8 * quarter : 8 * quarter + 8, :, 128 * m : 128 * m + 128].reshape(8, 128)
-                    for m in range(5)
-                ],
-                0,
-            )
-            for quarter in range(4)
-        ],
-        32,
-    )
-
-    def joined(first, second, last):
-        tiles = [parts[k][8 * first : 8 * first + 8] for k in range(4)]
-        tiles += [parts[k][8 * second : 8 * second + 8] for k in range(4)]
-        tiles.append(parts[last][32:40])
+    sides = []
+    for half in range(2):
+        rows = [
+            in_ref[8 * half : 8 * half + 8, :, 128 * m : 128 * m + 128].reshape(8, 128)
+            for m in range(WAVES)
+        ]
+        sides.append(jnp.concatenate(rows, 0))
+    sides = swapped(sides, 64)
+
+    def joined(start, last):
+        tiles = [
+            sides[k % 2][8 * (start + k // 2) : 8 * (start + k // 2) + 8] for k in range(8)
+        ]
+        tiles.append(sides[last][64:72])
         return jnp.concatenate([jnp.concatenate(tiles[3 * t : 3 * t + 3], 1) for t in range(3)], 0)
 
     ratio, root = ratio_of(lam_ref[...])
     scale = (1.0 / (N * N)) / root
-    run = joined(0, 1, 0)
+    run = joined(0, 0)
     for i in range(CELLS):
         run = run * ratio
         lines_ref[BLOCK * i : BLOCK * (i + 1), :] = run
         run = run + field_ref[BLOCK * i : BLOCK * (i + 1), :]
-    run = joined(2, 3, 1)
+    run = joined(4, 1)
     for i in range(CELLS - 1, -1, -1):
         at = slice(BLOCK * i, BLOCK * (i + 1))
         run = run * ratio + field_ref[at, :]
@@ -233,11 +265,20 @@
     send_lines(lines_ref[...], high_ref, low_ref, out_ref, block_of)
 
 
-def last_kernel(in_ref, high_ref, low_ref, out_ref, lines_ref):
+def last_kernel(in_ref, high_ref, low_ref, out_ref, lines_ref, result_ref, sems):
     received_lines(in_ref, lines_ref)
     table = (high_ref[...], low_ref[...])
-    result = product(halves(lines_ref[...]), table, ((1,), (0,)))
-    out_ref[...] = result.reshape(CELLS, BLOCK, N)
+    cells = CELLS // PARTS
+    copies = []
+    for part in range(PARTS):
+        rows = halves(lines_ref[BLOCK * cells * part : BLOCK * cells * (part + 1), :])
+        result = product(rows, table, ((1,), (0,)))
+        at = pl.ds(cells * part, cells)
+        result_ref[at] = result.reshape(cells, BLOCK, N)
+        copies.append(pltpu.make_async_copy(result_ref.at[at], out_ref.at[at], sems.at[part]))
+        copies[-1].start()
+    for copy in copies:
+        copy.wait()
 
 
 def call(kernel, name, **kwargs):
@@ -271,6 +312,11 @@
 
 def exchange(x):
     return lax.all_to_all(x, ("rep", "col"), 0, 0, tiled=True)
+
+
+def arc_exchange(x):
+    arcs = [list(range(ARC)), list(range(ARC, ROW))]
+    return lax.all_to_all(x, "row", 0, 0, axis_index_groups=arcs, tiled=True)
 
 
 def body(sources):
@@ -284,32 +330,46 @@
     third = lax.dynamic_slice_in_dim(eigen, (col * REP + rep) * BLOCK, BLOCK)
     lam = third[:, None] + eigen[None, :] + SHIFT
     packed = shaped(GROUP, 8 * PACKED, 128)
-    waves = shaped(ROW, 1, 640)
+    waves = shaped(ARC, 1, 128 * WAVES)
     modes = call(first_kernel, "first", out_shape=packed)(mine, got, high, low)
-    modes, lam, place = lax.optimization_barrier((modes, lam, row.reshape(1)))
+    place = (row % ARC).reshape(1)
+    modes, lam, place = lax.optimization_barrier((modes, lam, place))
     field, sums, step = call(
         second_kernel,
         "second",
-        out_shape=(shaped(LINES, N), waves, shaped(3 * ROW, 128)),
+        out_shape=(shaped(LINES, N), waves, shaped(5 * ARC, 128)),
         scratch_shapes=[lines_scratch()],
     )(exchange(modes), lam, high, low)
-    sums = lax.all_to_all(sums, "row", 0, 0, tiled=True)
     vmem = pl.BlockSpec(memory_space=pltpu.VMEM)
+    smem = pl.BlockSpec(memory_space=pltpu.SMEM)
+    sums, whole = call(
+        arc_kernel,
+        "arc",
+        in_specs=[smem, vmem, vmem],
+        out_shape=(shaped(ARC, 128 * WAVES), shaped(1, 128 * WAVES)),
+    )(place, arc_exchange(sums), step)
+    other = lax.ppermute(whole, "row", [(i, (i + ARC) % ROW) for i in range(ROW)])
     sums = call(
         ring_kernel,
         "ring",
-        in_specs=[pl.BlockSpec(memory_space=pltpu.SMEM), vmem, vmem],
+        in_specs=[smem, vmem, vmem, vmem, vmem],
         out_shape=waves,
-    )(place, sums, step)
-    sums = lax.all_to_all(sums, "row", 0, 0, tiled=True)
+    )(place, sums, whole, other, step)
+    sums = arc_exchange(sums)
     lines = call(third_kernel, "third", out_shape=packed, scratch_shapes=[lines_scratch()])(
         field, sums, lam, high, low
     )
     result = call(
         last_kernel,
         "last",
+        in_specs=[vmem, vmem, vmem],
+        out_specs=pl.BlockSpec(memory_space=pl.ANY),
         out_shape=shaped(CELLS, BLOCK, N),
-        scratch_shapes=[lines_scratch()],
+        scratch_shapes=[
+            lines_scratch(),
+            pltpu.VMEM((CELLS, BLOCK, N), F32),
+            pltpu.SemaphoreType.DMA((PARTS,)),
+        ],
     )(exchange(lines), high, low)
     return jnp.transpose(result, (1, 0, 2))
 

time: 92.6 us -> 90.4 us (0.976)
  blocking collectives: 76.1 us -> 68.1 us
  starting transfers between devices: 8.75 us -> 13.1 us
  waiting for transfers between devices: 0.54 us -> 2.03 us
    all_to_all x2, blocking collectives: 48.2 us -> 39.5 us  [arc_exchange(): return lax.all_to_all(x, 'row', 0, 0, axis_index_groups=arcs, tiled=True)]
    ppermute x0 -> x1, starting transfers between devices: none -> 4.35 us  [body(): lax.ppermute(whole, 'row', [(i, (i + ARC) % ROW) for i in range(ROW)])]
    ppermute x0 -> x1, waiting for transfers between devices: none -> 1.5 us  [body(): lax.ppermute(whole, 'row', [(i, (i + ARC) % ROW) for i in range(ROW)])]
    pallas_call x2 -> x3, Pallas kernels: 1.92 us -> 2 us  [the longest x1 1.82 us: body(): call(last_kernel, 'last', in_specs=[vmem, vmem, vmem], out_specs=pl.Block...]
  transfers between devices with their start and end apart: 1 -> 2, of which waited for: 1 -> 2; matrix products, arithmetic and copies ran while one was open for 0% -> 0% of each run, Pallas kernels for 0% -> 0%
where the time goes in v3:
time: 90.4 us; the launch traced here: 90.1 us
  blocking collectives  68.1 us (75%)
  starting transfers between devices  13.1 us (14%)
  Pallas kernels  4.84 us (5%)
  waiting for transfers between devices  2.03 us (2%)
  local copies, waits for them, and re-layouts  1.83 us (2%)
    all_to_all x2, blocking collectives, arc_exchange(): return lax.all_to_all(x, 'row', 0, 0, axis_index_groups=arcs, tiled=True)  39.5 us
    all_to_all x2, blocking collectives, exchange(): return lax.all_to_all(x, ('rep', 'col'), 0, 0, tiled=True)  28.6 us
    ppermute x1, starting transfers between devices, body(): got = lax.ppermute(other, 'rep', [(0, 1), (1, 0)])  8.75 us
    ppermute x1, starting transfers between devices, body(): lax.ppermute(whole, 'row', [(i, (i + ARC) % ROW) for i in range(ROW)])  4.35 us
    pallas_call x1, Pallas kernels, body(): call(last_kernel, 'last', in_specs=[vmem, vmem, vmem], out_specs=pl.Block...  1.82 us
  transfers between devices with their start and end apart: 2, of which 2 were waited for; matrix products, arithmetic and copies ran while one was open for 0% of the time, Pallas kernels for 0%

profile of v3, /device:TPU:1, one launch (start us, length us, event | category | flops | bytes accessed | tf_op | source)
XLA Modules:
  0.0 90.1 jit_solution(15642712547198380517)
XLA Ops:
  0.0 0.0 copy-start.2
  0.0 1.1 %dynamic-slice_bitcast_fusion = f32[12,24,384]{2,1,0:T(8,128)S(1)} fusion(f32[1,48,12,384]{3,1,2,0:T(8,128)} %param.4, s32[]{:T(128)S(6)} %select_n.13), kind=kLoop, calls=%fused_computation | loop fusion | bytes 884740 | tf_op jit(solution)/shard_map/dynamic_slice | solution.py:327
  1.1 8.7 %collective-permute-start = (f32[12,24,384]{2,1,0:T(8,128)S(1)}, f32[12,24,384]{2,1,0:T(8,128)S(1)}, u32[]{:S(2)}, u32[]{:S(2)}) collective-permute-start(f32[12,24,384]{2,1,0:T(8,128)S(1)} %dynamic-slice_bitcast_fusion), channel_id=1, source_target_pairs={{0,256},{256,0},{1,257},{257,1},{2,258},{258,2},{3,259},{259,3},{4... | collective-permute-start | bytes 1327112 | tf_op jit(solution)/shard_map/ppermute | solution.py:328
  9.9 0.0 copy-done.2
  9.9 0.0 copy-start.3
  9.9 0.0 copy-start
  9.9 0.0 copy-start.1
  10.0 0.6 copy-done.3
  10.6 0.1 dynamic_slice.7
  10.7 0.1 add_add_fusion.lam_ref
  10.7 0.5 collective-permute-done.got_ref
  11.3 0.0 copy-done
  11.3 0.0 copy-done.1
  11.3 0.8 first.1
  12.1 12.7 %all_to_all.20.in_ref = f32[16,56,128]{2,1,0:T(8,128)S(1)} all-to-all(f32[16,56,128]{2,1,0:T(8,128)S(1)} %first.1), channel_id=1, replica_groups=mesh['rep'=2,'row'=32,'col'=8] {'rep','col'}, dimensions={0} | all-to-all | bytes 917504 | tf_op jit(solution)/shard_map/all_to_all | solution.py:314
  24.8 1.1 %second.1 = (f32[288,384]{1,0:T(8,128)S(1)}, f32[16,1,1152]{2,1,0:T(1,128)S(1)}, f32[80,128]{1,0:T(8,128)S(1)}) custom-call(f32[16,56,128]{2,1,0:T(8,128)S(1)} %all_to_all.20.in_ref, f32[24,384]{1,0:T(8,128)S(1)} %add_add_fusion.lam_ref, bf16[384,384]{1,0:T(8,128)(2,1)S(1)} %copy-done, bf16[384,384]{1,0:T(8,128)(2,1)S(1)} %copy-done.1), custom_call_target="tpu_custom_call" | custom-call | tf_op jit(solution)/shard_map/second/pallas_call | solution.py:337
  25.9 23.9 %all_to_all.21.in_ref = f32[16,1,1152]{2,1,0:T(1,128)S(1)} all-to-all(f32[16,1,1152]{2,1,0:T(1,128)S(1)} %get-tuple-element.17), channel_id=1, replica_groups={{0,8,16,24,32,40,48,56,64,72,80,88,96,104,112,120},{128,136,144,152,160..., dimensions={0} | all-to-all | bytes 147456 | tf_op jit(solution)/shard_map/all_to_all | solution.py:319
  49.8 0.1 arc.1
  49.9 4.3 %collective-permute-start.1 = (f32[1,1152]{1,0:T(1,128)S(1)}, f32[1,1152]{1,0:T(1,128)S(1)}, u32[]{:S(2)}, u32[]{:S(2)}) collective-permute-start(f32[1,1152]{1,0:T(1,128)S(1)} %get-tuple-element.20.whole_ref), channel_id=1, source_target_pairs={{0,128},{8,136},{16,144},{24,152},{32,160},{40,168},{48,176},{56,1... | collective-permute-start | bytes 13832 | tf_op jit(solution)/shard_map/ppermute | solution.py:351
  54.2 1.5 %collective-permute-done.1.other_ref = f32[1,1152]{1,0:T(1,128)S(1)} collective-permute-done((f32[1,1152]{1,0:T(1,128)S(1)}, f32[1,1152]{1,0:T(1,128)S(1)}, u32[]{:S(2)}, u32[]{:S(2)}) %collective-permute-start.1) | collective-permute-done | bytes 4640 | tf_op jit(solution)/shard_map/ppermute | solution.py:351
  55.7 0.1 ring.1
  55.8 15.6 %all_to_all.22.in_ref = f32[16,1,1152]{2,1,0:T(1,128)S(1)} all-to-all(f32[16,1,1152]{2,1,0:T(1,128)S(1)} %ring.1), channel_id=1, replica_groups={{0,8,16,24,32,40,48,56,64,72,80,88,96,104,112,120},{128,136,144,152,160..., dimensions={0} | all-to-all | bytes 147456 | tf_op jit(solution)/shard_map/all_to_all | solution.py:319
  71.5 0.9 %third.1 = f32[16,56,128]{2,1,0:T(8,128)S(1)} custom-call(f32[288,384]{1,0:T(8,128)S(1)} %get-tuple-element.15.field_ref, f32[16,1,1152]{2,1,0:T(1,128)S(1)} %all_to_all.22.in_ref, f32[24,384]{1,0:T(8,128)S(1)} %add_add_fusion.lam_ref, bf16[384,384]{1,0:T(8,128)(2,1)S(1)} %copy-done, bf16[384,384]{1,0:T(8,128)(2,1)S(1)} %copy-done.1), custom_call_target="tpu_custom_call" | custom-call | tf_op jit(solution)/shard_map/third/pallas_call | solution.py:359
  72.4 15.9 %all_to_all.23.in_ref = f32[16,56,128]{2,1,0:T(8,128)S(1)} all-to-all(f32[16,56,128]{2,1,0:T(8,128)S(1)} %third.1), channel_id=1, replica_groups=mesh['rep'=2,'row'=32,'col'=8] {'rep','col'}, dimensions={0} | all-to-all | bytes 917504 | tf_op jit(solution)/shard_map/all_to_all | solution.py:314
  88.2 1.8 %last.1 = f32[12,24,384]{2,1,0:T(8,128)} custom-call(f32[16,56,128]{2,1,0:T(8,128)S(1)} %all_to_all.23.in_ref, bf16[384,384]{1,0:T(8,128)(2,1)S(1)} %copy-done, bf16[384,384]{1,0:T(8,128)(2,1)S(1)} %copy-done.1), custom_call_target="tpu_custom_call" | custom-call | tf_op jit(solution)/shard_map/last/pallas_call | solution.py:362
  (1 shorter events, 0.0 us)
Async XLA Ops:
  0.0 9.9 %copy-start.2 = (f32[1,48,12,384]{3,1,2,0:T(8,128)S(1)}, f32[1,48,12,384]{3,1,2,0:T(8,128)}, u32[]{:S(2)}) copy-start(f32[1,48,12,384]{3,1,2,0:T(8,128)} %param.4) | copy-start | bytes 2654212
  1.1 10.2 %collective-permute-start = (f32[12,24,384]{2,1,0:T(8,128)S(1)}, f32[12,24,384]{2,1,0:T(8,128)S(1)}, u32[]{:S(2)}, u32[]{:S(2)}) collective-permute-start(f32[12,24,384]{2,1,0:T(8,128)S(1)} %dynamic-slice_bitcast_fusion), channel_id=1, source_target_pairs={{0,256},{256,0},{1,257},{257,1},{2,258},{258,2},{3,259},{259,3},{4... | collective-permute-start | bytes 1327112 | tf_op jit(solution)/shard_map/ppermute | solution.py:328
  9.9 0.7 copy-start.3
  9.9 1.4 %copy-start = (bf16[384,384]{1,0:T(8,128)(2,1)S(1)}, bf16[384,384]{1,0:T(8,128)(2,1)}, u32[]{:S(2)}) copy-start(bf16[384,384]{1,0:T(8,128)(2,1)} %constant.48.clone.high_ref) | copy-start | bytes 884740
  9.9 1.4 %copy-start.1 = (bf16[384,384]{1,0:T(8,128)(2,1)S(1)}, bf16[384,384]{1,0:T(8,128)(2,1)}, u32[]{:S(2)}) copy-start(bf16[384,384]{1,0:T(8,128)(2,1)} %constant.49.clone.low_ref) | copy-start | bytes 884740
  49.9 5.9 %collective-permute-start.1 = (f32[1,1152]{1,0:T(1,128)S(1)}, f32[1,1152]{1,0:T(1,128)S(1)}, u32[]{:S(2)}, u32[]{:S(2)}) collective-permute-start(f32[1,1152]{1,0:T(1,128)S(1)} %get-tuple-element.20.whole_ref), channel_id=1, source_target_pairs={{0,128},{8,136},{16,144},{24,152},{32,160},{40,168},{48,176},{56,1... | collective-permute-start | bytes 13832 | tf_op jit(solution)/shard_map/ppermute | solution.py:351

commit v4 on v2

v4 whole, which is shorter than its diff:
```python
import ml_dtypes
import numpy as np

import jax
import jax.numpy as jnp
from jax import lax
from jax.experimental import pallas as pl
from jax.experimental.pallas import tpu as pltpu
from jax.sharding import Mesh
from jax.sharding import PartitionSpec as P

N = 384
SHIFT = 0.001
REP, COL, ROW = 2, 8, 32
GROUP = REP * COL
BLOCK = N // GROUP
CELLS = N // ROW
LINES = CELLS * BLOCK
TILES = BLOCK // 8
PACKED = 2 * TILES + 1
PARTS, PAIR = 4, 2
RING = ROW // PARTS
VMEM_BYTES = 12 * 2**20
F32 = jnp.float32
BF16 = jnp.bfloat16


def block_of(member):
    return member % COL * REP + member // COL


def member_of(block):
    return block % REP * COL + block // REP


def tables():
    order = [
        BLOCK * block_of(member) + 8 * tile + low
        for tile in range(TILES)
        for member in range(GROUP)
        for low in range(8)
    ]
    turns = np.outer(np.asarray(order), np.arange(N)) % N
    angle = turns * (2.0 * np.pi / N)
    cas = np.cos(angle) + np.sin(angle)
    high = cas.astype(ml_dtypes.bfloat16)
    low = (cas - high.astype(np.float64)).astype(ml_dtypes.bfloat16)
    return high, low


def eigen_line():
    return (4.0 * np.sin(np.pi * np.arange(N) / N) ** 2).astype(np.float32)


def halves(x):
    high = x.astype(BF16)
    return high, (x - high.astype(F32)).astype(BF16)


def product(first, second, contract):
    dims = (contract, ((), ()))
    (fh, fl), (sh, sl) = first, second
    out = lax.dot_general(fl, sh, dims, preferred_element_type=F32)
    out += lax.dot_general(fh, sl, dims, preferred_element_type=F32)
    return out + lax.dot_general(fh, sh, dims, preferred_element_type=F32)


def lanes(shape):
    return lax.broadcasted_iota(jnp.int32, shape, 1)


def swapped(parts, width):
    parts = list(parts)
    lane = lanes(parts[0].shape)
    bit = 1
    while bit < len(parts):
        reach = width * bit
        upper = (lane & reach) != 0
        for i in range(len(parts)):
            if i & bit:
                continue
            a, b = parts[i], parts[i | bit]
            parts[i] = jnp.where(upper, pltpu.roll(b, reach, 1), a)
            parts[i | bit] = jnp.where(upper, b, pltpu.roll(a, 128 - reach, 1))
        bit *= 2
    return parts


def ratio_of(lam):
    root = jnp.sqrt(lam * (lam + 4.0))
    return 2.0 / (2.0 + lam + root), root


def send_tile(out_ref, member, piece, tile):
    for part in range(PARTS):
        out_ref[PARTS * member + part, piece] = tile[PAIR * part : PAIR * (part + 1), :]


def received(in_ref, member):
    parts = [in_ref[PARTS * member + part] for part in range(PARTS)]
    return jnp.concatenate(parts, 1).reshape(8 * PACKED, 128)


def unit_place(unit, tile):
    if unit < 32:
        return unit % 16, 8 * (2 * tile + unit // 16)
    return 4 * tile + unit - 32, 8 * (PACKED - 1)


def first_kernel(mine_ref, got_ref, high_ref, low_ref, out_ref):
    density = (mine_ref[...] + got_ref[...]).reshape(LINES, N)
    pad = jnp.zeros((N - LINES, N), BF16)
    lines = tuple(jnp.concatenate([part, pad], 0) for part in halves(density))
    modes = product((high_ref[...], low_ref[...]), lines, ((1,), (1,)))
    rows = 8 * GROUP
    lane = lanes((rows, 128))
    rest = modes[0:rows, 256:384]
    for tile in range(1, TILES):
        moved = pltpu.roll(modes[rows * tile : rows * (tile + 1), 256:384], 32 * tile, 1)
        rest = jnp.where(lane < 32 * tile, rest, moved)
    for member in range(GROUP):
        at = 8 * member
        for tile in range(TILES):
            row = rows * tile + at
            for half in range(2):
                piece = modes[row : row + 8, 128 * half : 128 * half + 128]
                send_tile(out_ref, member, 2 * tile + half, piece)
        send_tile(out_ref, member, PACKED - 1, rest[at : at + 8])


def second_kernel(
    in_ref, lam_ref, high_ref, low_ref, field_ref, right_ref, left_ref, waves_ref, lines_ref
):
    packed = swapped([received(in_ref, member) for member in range(GROUP)], 8)
    for unit in range(CELLS * TILES):
        cell, piece = unit // TILES, unit % TILES
        for tile in range(TILES):
            source, at = unit_place(unit, tile)
            to = BLOCK * cell + 8 * tile
            lanes_to = slice(128 * piece, 128 * piece + 128)
            lines_ref[to : to + 8, lanes_to] = packed[source][at : at + 8]
    table = (high_ref[...], low_ref[...])
    field_ref[...] = product(halves(lines_ref[...]), table, ((1,), (0,)))
    ratio, _ = ratio_of(lam_ref[...])
    right = field_ref[0:BLOCK, :]
    left = field_ref[LINES - BLOCK : LINES, :]
    for i in range(1, CELLS):
        right = right * ratio + field_ref[BLOCK * i : BLOCK * (i + 1), :]
        j = CELLS - 1 - i
        left = left * ratio + field_ref[BLOCK * j : BLOCK * (j + 1), :]
    right_ref[...] = right
    left_ref[...] = left
    step = chunk_step(ratio)
    lower = sublanes((8, N)) < 4
    for tile in range(TILES):
        at = slice(8 * tile, 8 * tile + 8)
        joined = jnp.where(
            lower,
            step[at] * right[at] + pltpu.roll(right[at], 4, 0),
            step[at] * left[at] + pltpu.roll(left[at], 4, 0),
        )
        for member in range(RING):
            waves_ref[member, at, :] = joined


def chunk_step(ratio):
    square = ratio * ratio
    fourth = square * square
    return fourth * fourth * fourth


def sublanes(shape):
    return lax.broadcasted_iota(jnp.int32, shape, 0)


def ring_inflow(place, waves_ref, at, step):
    pair = step * step
    zero = jnp.zeros((8, N), F32)
    sides = []
    for forward in (True, False):
        before, rest, whole, decay = zero, zero, zero, jnp.ones((8, N), F32)
        for k in range(RING):
            member = k if forward else RING - 1 - k
            wave = waves_ref[member, at, :]
            earlier = member < place if forward else member > place
            before = jnp.where(earlier, before * pair + wave, before)
            rest = jnp.where(earlier, rest, rest * pair + wave)
            whole = whole * pair + wave
            decay = jnp.where(earlier, decay * pair, decay)
        sides.append((before, rest, whole, decay))
    row = sublanes((8, N))
    before, rest, whole, decay = (jnp.where(row < 4, *both) for both in zip(*sides))
    first_arc = (row & 2) == 0
    other = jnp.where(first_arc, pltpu.roll(whole, 6, 0), pltpu.roll(whole, 2, 0))
    power = pair
    for _ in range(3):
        power = power * power
    return (before + decay * (other + power * rest)) / (1.0 - power * power)


def third_kernel(
    place_ref,
    field_ref,
    right_ref,
    left_ref,
    waves_ref,
    lam_ref,
    high_ref,
    low_ref,
    out_ref,
    lines_ref,
):
    ratio, root = ratio_of(lam_ref[...])
    step = chunk_step(ratio)
    lower = sublanes((8, N)) < 4
    forward, backward = [], []
    for tile in range(TILES):
        at = slice(8 * tile, 8 * tile + 8)
        inflow = ring_inflow(place_ref[0], waves_ref, at, step[at])
        turned = pltpu.roll(inflow, 4, 0)
        right = pltpu.roll(right_ref[at, :], 4, 0)
        left = pltpu.roll(left_ref[at, :], 4, 0)
        forward.append(jnp.where(lower, inflow, step[at] * turned + right))
        backward.append(jnp.where(lower, step[at] * turned + left, inflow))
    scale = (1.0 / (N * N)) / root
    run = jnp.concatenate(forward, 0)
    for i in range(CELLS):
        run = run * ratio
        lines_ref[BLOCK * i : BLOCK * (i + 1), :] = run
        run = run + field_ref[BLOCK * i : BLOCK * (i + 1), :]
    run = jnp.concatenate(backward, 0)
    for i in range(CELLS - 1, -1, -1):
        at = slice(BLOCK * i, BLOCK * (i + 1))
        run = run * ratio + field_ref[at, :]
        lines_ref[at, :] = (lines_ref[at, :] + run) * scale
    table = (high_ref[...], low_ref[...])
    lines_ref[...] = product(halves(lines_ref[...]), table, ((1,), (1,)))
    tiles = [[jnp.zeros((8, 128), F32)] * PACKED for _ in range(GROUP)]
    for unit in range(CELLS * TILES):
        cell, piece = unit // TILES, unit % TILES
        for tile in range(TILES):
            source, at = unit_place(unit, tile)
            row = BLOCK * cell + 8 * tile
            tiles[source][at // 8] = lines_ref[row : row + 8, 128 * piece : 128 * piece + 128]
    packed = swapped([jnp.concatenate(group, 0) for group in tiles], 8)
    for member in range(GROUP):
        slot = block_of(member)
        for piece in range(PACKED):
            send_tile(out_ref, slot, piece, packed[member][8 * piece : 8 * piece + 8])


def last_kernel(in_ref, high_ref, low_ref, out_ref, modes_ref):
    for member in range(GROUP):
        packed = received(in_ref, member)
        rest = packed[8 * (PACKED - 1) : 8 * PACKED]
        for tile in range(TILES):
            row = 8 * (GROUP * tile + member)
            for half in range(2):
                at = 8 * (2 * tile + half)
                modes_ref[row : row + 8, 128 * half : 128 * half + 128] = packed[at : at + 8]
            moved = rest if tile == 0 else pltpu.roll(rest, 128 - 32 * tile, 1)
            modes_ref[row : row + 8, 256:384] = moved
    table = (high_ref[...], low_ref[...])
    result = product(halves(modes_ref[...].T[0:LINES]), table, ((1,), (0,)))
    out_ref[...] = result.reshape(CELLS, BLOCK, N)


def call(kernel, name, **kwargs):
    params = pltpu.CompilerParams(vmem_limit_bytes=VMEM_BYTES)
    return pl.pallas_call(kernel, name=name, compiler_params=params, **kwargs)


def shaped(*shape):
    return jax.ShapeDtypeStruct(shape, F32)


def lines_scratch():
    return pltpu.VMEM((LINES, N), F32)


def copy_kernel(rep_ref, in_ref, out_ref):
    out_ref[...] = in_ref[...]


def own_half(part, rep):
    shape = (CELLS, BLOCK, N)
    grid_spec = pltpu.PrefetchScalarGridSpec(
        num_scalar_prefetch=1,
        grid=(1,),
        in_specs=[pl.BlockSpec(shape, lambda i, rep_ref: (0, rep_ref[0], 0))],
        out_specs=pl.BlockSpec(shape, lambda i, rep_ref: (0, 0, 0)),
    )
    out = shaped(*shape)
    return call(copy_kernel, "mine", grid_spec=grid_spec, out_shape=out)(rep.reshape(1), part)


def exchange(x):
    return lax.all_to_all(x, ("rep", "col", "zl", "xh"), 0, 0, tiled=True)


def body(sources):
    rep, col = lax.axis_index("rep"), lax.axis_index("col")
    part_index = lax.axis_index("zl") * 2 + lax.axis_index("xh")
    high, low = (jnp.asarray(part) for part in tables())
    part = jnp.transpose(sources[0], (1, 0, 2))
    mine = own_half(part, rep)
    other = lax.dynamic_slice_in_dim(part, (1 - rep) * BLOCK, BLOCK, 1)
    got = lax.ppermute(other, "rep", [(0, 1), (1, 0)])
    eigen = jnp.asarray(eigen_line())
    third = lax.dynamic_slice_in_dim(eigen, (col * REP + rep) * BLOCK, BLOCK)
    third = lax.dynamic_index_in_dim(third.reshape(TILES, PARTS, PAIR), part_index, 1)
    third = jnp.broadcast_to(third, (TILES, PARTS, PAIR)).reshape(BLOCK)
    lam = third[:, None] + eigen[None, :] + SHIFT
    packed = shaped(GROUP * PARTS, PACKED, PAIR, 128)
    modes = call(first_kernel, "first", out_shape=packed)(mine, got, high, low)
    place = lax.axis_index("zh").reshape(1)
    modes, lam, place = lax.optimization_barrier((modes, lam, place))
    side = shaped(BLOCK, N)
    field, right, left, waves = call(
        second_kernel,
        "second",
        out_shape=(shaped(LINES, N), side, side, shaped(RING, BLOCK, N)),
        scratch_shapes=[lines_scratch()],
    )(exchange(modes), lam, high, low)
    waves = lax.all_to_all(waves, "zh", 0, 0, tiled=True)
    vmem = pl.BlockSpec(memory_space=pltpu.VMEM)
    lines = call(
        third_kernel,
        "third",
        in_specs=[pl.BlockSpec(memory_space=pltpu.SMEM)] + [vmem] * 7,
        out_shape=packed,
        scratch_shapes=[lines_scratch()],
    )(place, field, right, left, waves, lam, high, low)
    result = call(
        last_kernel,
        "last",
        out_shape=shaped(CELLS, BLOCK, N),
        scratch_shapes=[pltpu.VMEM((N, N), F32)],
    )(exchange(lines), high, low)
    return jnp.transpose(result, (1, 0, 2))


def solution(mesh):
    devices = mesh.devices.reshape(REP, 2, RING, 2, COL)
    split = Mesh(devices, ("rep", "xh", "zh", "zl", "col"))
    row = ("xh", "zh", "zl")
    return jax.shard_map(
        body,
        mesh=split,
        in_specs=(P("rep", "col", row, None),),
        out_specs=P(("rep", "col"), row, None),
        check_vma=False,
    )
```

time: 92.6 us -> 84.9 us (0.917)
  blocking collectives: 76.1 us -> 67.8 us
  local copies, waits for them, and re-layouts: 1.83 us -> 3.11 us
    all_to_all x4 -> x3, blocking collectives: 76.1 us -> 67.8 us  [the longest x1 35.7 us: body(): waves = lax.all_to_all(waves, 'zh', 0, 0, tiled=True)]
    pallas_call x3 -> x2, Pallas kernels: 2.37 us -> 2.39 us  [the longest x1 1.33 us: body(): call(third_kernel, 'third', in_specs=[pl.BlockSpec(memory_space=pltpu.SME...]
  transfers between devices with their start and end apart: 1 -> 1, of which waited for: 1 -> 1; matrix products, arithmetic and copies ran while one was open for 0% -> 1% of each run, Pallas kernels for 0% -> 0%
where the time goes in v4:
time: 84.9 us; the launch traced here: 84.7 us
  blocking collectives  67.8 us (80%)
  starting transfers between devices  8.75 us (10%)
  Pallas kernels  4.71 us (6%)
  local copies, waits for them, and re-layouts  3.11 us (4%)
    all_to_all x1, blocking collectives, body(): waves = lax.all_to_all(waves, 'zh', 0, 0, tiled=True)  35.7 us
    all_to_all x2, blocking collectives, exchange(): return lax.all_to_all(x, ('rep', 'col', 'zl', 'xh'), 0, 0, tiled=True)  32.2 us
    ppermute x1, starting transfers between devices, body(): got = lax.ppermute(other, 'rep', [(0, 1), (1, 0)])  8.75 us
  transfers between devices with their start and end apart: 1, of which 1 were waited for; matrix products, arithmetic and copies ran while one was open for 1% of the time, Pallas kernels for 0%

profile of v4, /device:TPU:1, one launch (start us, length us, event | category | flops | bytes accessed | tf_op | source)
XLA Modules:
  0.0 84.7 jit_solution(8108081507935534404)
XLA Ops:
  0.0 0.0 copy-start.2
  0.0 1.1 %dynamic-slice_bitcast_fusion = f32[12,24,384]{2,1,0:T(8,128)S(1)} fusion(f32[1,48,12,384]{3,1,2,0:T(8,128)} %param.4, s32[]{:T(128)S(6)} %select_n.10), kind=kLoop, calls=%fused_computation | loop fusion | bytes 884740 | tf_op jit(solution)/shard_map/dynamic_slice | solution.py:307
  1.1 8.7 %collective-permute-start = (f32[12,24,384]{2,1,0:T(8,128)S(1)}, f32[12,24,384]{2,1,0:T(8,128)S(1)}, u32[]{:S(2)}, u32[]{:S(2)}) collective-permute-start(f32[12,24,384]{2,1,0:T(8,128)S(1)} %dynamic-slice_bitcast_fusion), channel_id=1, source_target_pairs={{0,256},{256,0},{1,257},{257,1},{2,258},{258,2},{3,259},{259,3},{4... | collective-permute-start | bytes 1327112 | tf_op jit(solution)/shard_map/ppermute | solution.py:308
  9.9 0.0 copy-start.3
  9.9 0.7 copy-done.3
  10.6 0.1 dynamic_slice.11
  10.7 0.1 reshape.16
  10.8 0.1 copy.7
  10.8 0.1 copy.8
  10.9 0.1 add.42
  11.1 0.0 copy-done.2
  11.1 0.0 copy-start
  11.1 0.0 copy-start.1
  11.1 0.1 add_add_fusion.lam_ref
  11.2 0.1 collective-permute-done.got_ref
  11.3 0.7 copy-done
  12.0 0.1 copy-done.1
  12.1 0.8 first.1
  12.9 15.1 %all_to_all.15.in_ref = f32[64,7,2,128]{3,2,1,0:T(2,128)S(1)} all-to-all(f32[64,7,2,128]{3,2,1,0:T(2,128)S(1)} %first.1), channel_id=1, replica_groups=mesh['rep'=2,'xh'=2,'zh'=8,'zl'=2,'col'=8] {'rep','col','zl','xh'}, dimensions={0} | all-to-all | bytes 917504 | tf_op jit(solution)/shard_map/all_to_all | solution.py:298
  28.0 1.1 %second.1 = (f32[288,384]{1,0:T(8,128)S(1)}, f32[24,384]{1,0:T(8,128)S(1)}, f32[24,384]{1,0:T(8,128)S(1)}, f32[8,24,384]{2,1,0:T(8,128)S(1)}) custom-call(f32[64,7,2,128]{3,2,1,0:T(2,128)S(1)} %all_to_all.15.in_ref, f32[24,384]{1,0:T(8,128)S(1)} %add_add_fusion.lam_ref, bf16[384,384]{1,0:T(8,128)(2,1)S(1)} %copy-done, bf16[384,384]{1,0:T(8,128)(2,1)S(1)} %copy-done.1), custom_call_target="tpu_custom_call" | custom-call | tf_op jit(solution)/shard_map/second/pallas_call | solution.py:319
  29.0 35.7 %all_to_all.16.waves_ref = f32[8,24,384]{2,1,0:T(8,128)S(1)} all-to-all(f32[8,24,384]{2,1,0:T(8,128)S(1)} %get-tuple-element.18), channel_id=1, replica_groups=mesh['rep'=2,'xh'=2,'zh'=8,'zl'=2,'col'=8] {'zh'}, dimensions={0} | all-to-all | bytes 589824 | tf_op jit(solution)/shard_map/all_to_all | solution.py:325
  64.7 1.3 %third.1 = f32[64,7,2,128]{3,2,1,0:T(2,128)S(1)} custom-call(s32[1]{0:T(128)} %bitcast.6.place_ref, f32[288,384]{1,0:T(8,128)S(1)} %get-tuple-element.15.field_ref, f32[24,384]{1,0:T(8,128)S(1)} %get-tuple-element.16.right_ref, f32[24,384]{1,0:T(8,128)S(1)} %get-tuple-element.17.left_ref, f32[8,24,384]{2,1,0:T(8,128)S(1)} %all_to_all.16.waves_ref, ...), custom_call_target="tpu_custom_call" | custom-call | tf_op jit(solution)/shard_map/third/pallas_call | solution.py:327
  66.0 17.1 %all_to_all.17.in_ref = f32[64,7,2,128]{3,2,1,0:T(2,128)S(1)} all-to-all(f32[64,7,2,128]{3,2,1,0:T(2,128)S(1)} %third.1), channel_id=1, replica_groups=mesh['rep'=2,'xh'=2,'zh'=8,'zl'=2,'col'=8] {'rep','col','zl','xh'}, dimensions={0} | all-to-all | bytes 917504 | tf_op jit(solution)/shard_map/all_to_all | solution.py:298
  83.1 1.5 %last.1 = f32[12,24,384]{2,1,0:T(8,128)} custom-call(f32[64,7,2,128]{3,2,1,0:T(2,128)S(1)} %all_to_all.17.in_ref, bf16[384,384]{1,0:T(8,128)(2,1)S(1)} %copy-done, bf16[384,384]{1,0:T(8,128)(2,1)S(1)} %copy-done.1), custom_call_target="tpu_custom_call" | custom-call | tf_op jit(solution)/shard_map/last/pallas_call | solution.py:334
  (3 shorter events, 0.0 us)
Async XLA Ops:
  0.0 11.1 %copy-start.2 = (f32[1,48,12,384]{3,1,2,0:T(8,128)S(1)}, f32[1,48,12,384]{3,1,2,0:T(8,128)}, u32[]{:S(2)}) copy-start(f32[1,48,12,384]{3,1,2,0:T(8,128)} %param.4) | copy-start | bytes 2654212
  1.1 10.2 %collective-permute-start = (f32[12,24,384]{2,1,0:T(8,128)S(1)}, f32[12,24,384]{2,1,0:T(8,128)S(1)}, u32[]{:S(2)}, u32[]{:S(2)}) collective-permute-start(f32[12,24,384]{2,1,0:T(8,128)S(1)} %dynamic-slice_bitcast_fusion), channel_id=1, source_target_pairs={{0,256},{256,0},{1,257},{257,1},{2,258},{258,2},{3,259},{259,3},{4... | collective-permute-start | bytes 1327112 | tf_op jit(solution)/shard_map/ppermute | solution.py:308
  9.9 0.7 copy-start.3
  11.1 1.0 %copy-start = (bf16[384,384]{1,0:T(8,128)(2,1)S(1)}, bf16[384,384]{1,0:T(8,128)(2,1)}, u32[]{:S(2)}) copy-start(bf16[384,384]{1,0:T(8,128)(2,1)} %constant.46.clone.high_ref) | copy-start | bytes 884740
  11.1 1.0 %copy-start.1 = (bf16[384,384]{1,0:T(8,128)(2,1)S(1)}, bf16[384,384]{1,0:T(8,128)(2,1)}, u32[]{:S(2)}) copy-start(bf16[384,384]{1,0:T(8,128)(2,1)} %constant.47.clone.low_ref) | copy-start | bytes 884740

commit v5 on v4

--- a/solution.py
+++ b/solution.py
@@ -25,12 +25,13 @@
 BF16 = jnp.bfloat16
 
 
+def member_at(rep, col):
+    return col % 4 * 4 + rep * 2 + col // 4
+
+
 def block_of(member):
-    return member % COL * REP + member // COL
-
-
-def member_of(block):
-    return block % REP * COL + block // REP
+    rep, col = member // 2 % 2, member % 2 * 4 + member // 4
+    return col * REP + rep
 
 
 def tables():
@@ -50,6 +51,20 @@
 
 def eigen_line():
     return (4.0 * np.sin(np.pi * np.arange(N) / N) ** 2).astype(np.float32)
+
+
+def third_eigen():
+    rows = [
+        [
+            BLOCK * block_of(member) + 8 * tile + PAIR * part + low
+            for tile in range(TILES)
+            for _ in range(PARTS)
+            for low in range(PAIR)
+        ]
+        for member in range(GROUP)
+        for part in range(PARTS)
+    ]
+    return eigen_line()[np.asarray(rows)]
 
 
 def halves(x):
@@ -91,13 +106,14 @@
     return 2.0 / (2.0 + lam + root), root
 
 
-def send_tile(out_ref, member, piece, tile):
+def send_tile(out_ref, member, piece, tile, twist=0):
     for part in range(PARTS):
-        out_ref[PARTS * member + part, piece] = tile[PAIR * part : PAIR * (part + 1), :]
-
-
-def received(in_ref, member):
-    parts = [in_ref[PARTS * member + part] for part in range(PARTS)]
+        slot = GROUP * (part ^ twist) + member
+        out_ref[slot, piece] = tile[PAIR * part : PAIR * (part + 1), :]
+
+
+def received(in_ref, member, twist=0):
+    parts = [in_ref[GROUP * (part ^ twist) + member] for part in range(PARTS)]
     return jnp.concatenate(parts, 1).reshape(8 * PACKED, 128)
 
 
@@ -107,7 +123,7 @@
     return 4 * tile + unit - 32, 8 * (PACKED - 1)
 
 
-def first_kernel(mine_ref, got_ref, high_ref, low_ref, out_ref):
+def first_kernel(twist_ref, mine_ref, got_ref, high_ref, low_ref, out_ref):
     density = (mine_ref[...] + got_ref[...]).reshape(LINES, N)
     pad = jnp.zeros((N - LINES, N), BF16)
     lines = tuple(jnp.concatenate([part, pad], 0) for part in halves(density))
@@ -124,8 +140,8 @@
             row = rows * tile + at
             for half in range(2):
                 piece = modes[row : row + 8, 128 * half : 128 * half + 128]
-                send_tile(out_ref, member, 2 * tile + half, piece)
-        send_tile(out_ref, member, PACKED - 1, rest[at : at + 8])
+                send_tile(out_ref, member, 2 * tile + half, piece, twist_ref[0])
+        send_tile(out_ref, member, PACKED - 1, rest[at : at + 8], twist_ref[0])
 
 
 def second_kernel(
@@ -244,14 +260,14 @@
             tiles[source][at // 8] = lines_ref[row : row + 8, 128 * piece : 128 * piece + 128]
     packed = swapped([jnp.concatenate(group, 0) for group in tiles], 8)
     for member in range(GROUP):
-        slot = block_of(member)
+        slot = member_at(*divmod(block_of(member), COL))
         for piece in range(PACKED):
             send_tile(out_ref, slot, piece, packed[member][8 * piece : 8 * piece + 8])
 
 
-def last_kernel(in_ref, high_ref, low_ref, out_ref, modes_ref):
+def last_kernel(twist_ref, in_ref, high_ref, low_ref, out_ref, modes_ref):
     for member in range(GROUP):
-        packed = received(in_ref, member)
+        packed = received(in_ref, member, twist_ref[0])
         rest = packed[8 * (PACKED - 1) : 8 * PACKED]
         for tile in range(TILES):
             row = 8 * (GROUP * tile + member)
@@ -295,26 +311,36 @@
 
 
 def exchange(x):
-    return lax.all_to_all(x, ("rep", "col", "zl", "xh"), 0, 0, tiled=True)
+    return lax.all_to_all(x, ("zl", "xh", "y", "rep", "xl"), 0, 0, tiled=True)
+
+
+def ring_exchange(x):
+    rings = [[2 * k + (half ^ (k // (RING // 2))) for k in range(RING)] for half in range(2)]
+    return lax.all_to_all(x, ("zh", "zl"), 0, 0, axis_index_groups=rings, tiled=True)
 
 
 def body(sources):
-    rep, col = lax.axis_index("rep"), lax.axis_index("col")
-    part_index = lax.axis_index("zl") * 2 + lax.axis_index("xh")
+    rep, col = lax.axis_index("rep"), lax.axis_index("xl") * 4 + lax.axis_index("y")
+    place = lax.axis_index("zh")
+    twist = 2 * (place // (RING // 2))
+    part_index = (lax.axis_index("zl") * 2 + lax.axis_index("xh")) ^ twist
     high, low = (jnp.asarray(part) for part in tables())
     part = jnp.transpose(sources[0], (1, 0, 2))
     mine = own_half(part, rep)
     other = lax.dynamic_slice_in_dim(part, (1 - rep) * BLOCK, BLOCK, 1)
     got = lax.ppermute(other, "rep", [(0, 1), (1, 0)])
     eigen = jnp.asarray(eigen_line())
-    third = lax.dynamic_slice_in_dim(eigen, (col * REP + rep) * BLOCK, BLOCK)
-    third = lax.dynamic_index_in_dim(third.reshape(TILES, PARTS, PAIR), part_index, 1)
-    third = jnp.broadcast_to(third, (TILES, PARTS, PAIR)).reshape(BLOCK)
+    third = jnp.asarray(third_eigen())
+    third = lax.dynamic_index_in_dim(third, member_at(rep, col) * PARTS + part_index, keepdims=False)
     lam = third[:, None] + eigen[None, :] + SHIFT
     packed = shaped(GROUP * PARTS, PACKED, PAIR, 128)
-    modes = call(first_kernel, "first", out_shape=packed)(mine, got, high, low)
-    place = lax.axis_index("zh").reshape(1)
-    modes, lam, place = lax.optimization_barrier((modes, lam, place))
+    vmem = pl.BlockSpec(memory_space=pltpu.VMEM)
+    smem = pl.BlockSpec(memory_space=pltpu.SMEM)
+    place, twist = place.reshape(1), twist.reshape(1)
+    modes = call(first_kernel, "first", in_specs=[smem] + [vmem] * 4, out_shape=packed)(
+        twist, mine, got, high, low
+    )
+    modes, lam, place, twist = lax.optimization_barrier((modes, lam, place, twist))
     side = shaped(BLOCK, N)
     field, right, left, waves = call(
         second_kernel,
@@ -322,32 +348,32 @@
         out_shape=(shaped(LINES, N), side, side, shaped(RING, BLOCK, N)),
         scratch_shapes=[lines_scratch()],
     )(exchange(modes), lam, high, low)
-    waves = lax.all_to_all(waves, "zh", 0, 0, tiled=True)
-    vmem = pl.BlockSpec(memory_space=pltpu.VMEM)
+    waves = ring_exchange(waves)
     lines = call(
         third_kernel,
         "third",
-        in_specs=[pl.BlockSpec(memory_space=pltpu.SMEM)] + [vmem] * 7,
+        in_specs=[smem] + [vmem] * 7,
         out_shape=packed,
         scratch_shapes=[lines_scratch()],
     )(place, field, right, left, waves, lam, high, low)
     result = call(
         last_kernel,
         "last",
+        in_specs=[smem] + [vmem] * 3,
         out_shape=shaped(CELLS, BLOCK, N),
         scratch_shapes=[pltpu.VMEM((N, N), F32)],
-    )(exchange(lines), high, low)
+    )(twist, exchange(lines), high, low)
     return jnp.transpose(result, (1, 0, 2))
 
 
 def solution(mesh):
-    devices = mesh.devices.reshape(REP, 2, RING, 2, COL)
-    split = Mesh(devices, ("rep", "xh", "zh", "zl", "col"))
-    row = ("xh", "zh", "zl")
+    devices = mesh.devices.reshape(REP, 2, RING, 2, 2, 4)
+    split = Mesh(devices, ("rep", "xh", "zh", "zl", "xl", "y"))
+    row, col = ("xh", "zh", "zl"), ("xl", "y")
     return jax.shard_map(
         body,
         mesh=split,
-        in_specs=(P("rep", "col", row, None),),
-        out_specs=P(("rep", "col"), row, None),
+        in_specs=(P("rep", col, row, None),),
+        out_specs=P(("rep", *col), row, None),
         check_vma=False,
     )

time: 84.9 us -> 84.2 us (level)
  local copies, waits for them, and re-layouts: 3.11 us -> 1.9 us
    unnamed x8, local copies, waits for them, and re-layouts: 1.53 us -> 0.02 us
where the time goes in v5:
time: 84.2 us; the launch traced here: 84 us
  blocking collectives  67.7 us (80%)
  starting transfers between devices  8.75 us (10%)
  Pallas kernels  4.93 us (6%)
  local copies, waits for them, and re-layouts  1.9 us (2%)
    all_to_all x2, blocking collectives, exchange(): return lax.all_to_all(x, ('zl', 'xh', 'y', 'rep', 'xl'), 0, 0, tiled=True)  39.9 us
    all_to_all x1, blocking collectives, ring_exchange(): lax.all_to_all(x, ('zh', 'zl'), 0, 0, axis_index_groups=rings, tiled=True)  27.8 us
    ppermute x1, starting transfers between devices, body(): got = lax.ppermute(other, 'rep', [(0, 1), (1, 0)])  8.75 us
  transfers between devices with their start and end apart: 1, of which 1 were waited for; matrix products, arithmetic and copies ran while one was open for 1% of the time, Pallas kernels for 0%

profile of v5, /device:TPU:1, one launch (start us, length us, event | category | flops | bytes accessed | tf_op | source)
XLA Modules:
  0.0 84.0 jit_solution(12929004685085006904)
XLA Ops:
  0.0 0.0 copy-start.2
  0.0 1.1 %dynamic-slice_bitcast_fusion = f32[12,24,384]{2,1,0:T(8,128)S(1)} fusion(f32[1,48,12,384]{3,1,2,0:T(8,128)} %param.5, s32[]{:T(128)S(6)} %select_n.22), kind=kLoop, calls=%fused_computation | loop fusion | bytes 884740 | tf_op jit(solution)/shard_map/dynamic_slice | solution.py:330
  1.1 8.7 %collective-permute-start = (f32[12,24,384]{2,1,0:T(8,128)S(1)}, f32[12,24,384]{2,1,0:T(8,128)S(1)}, u32[]{:S(2)}, u32[]{:S(2)}) collective-permute-start(f32[12,24,384]{2,1,0:T(8,128)S(1)} %dynamic-slice_bitcast_fusion), channel_id=1, source_target_pairs={{0,256},{256,0},{1,257},{257,1},{2,258},{258,2},{3,259},{259,3},{4... | collective-permute-start | bytes 1327112 | tf_op jit(solution)/shard_map/ppermute | solution.py:331
  9.9 0.0 copy-done.2
  9.9 0.0 copy-start
  10.0 0.0 copy-start.1
  10.0 0.0 copy-start.3
  10.0 0.8 dynamic-slice_bitcast_fusion.1
  10.8 0.0 copy-done.3
  10.8 0.1 add_add_fusion.lam_ref
  10.9 0.4 collective-permute-done.got_ref
  11.3 0.0 copy-done
  11.3 0.0 copy-done.1
  11.3 1.0 %first.1 = f32[64,7,2,128]{3,2,1,0:T(2,128)S(1)} custom-call(s32[1]{0:T(128)} %bitcast.twist_ref, f32[12,24,384]{2,1,0:T(8,128)S(1)} %mine.1.mine_ref, f32[12,24,384]{2,1,0:T(8,128)S(1)} %collective-permute-done.got_ref, bf16[384,384]{1,0:T(8,128)(2,1)S(1)} %copy-done, bf16[384,384]{1,0:T(8,128)(2,1)S(1)} %copy-done.1), custom_call_target="tpu_custom_call" | custom-call | tf_op jit(solution)/shard_map/first/pallas_call | solution.py:340
  12.3 15.4 %all_to_all.15.in_ref = f32[64,7,2,128]{3,2,1,0:T(2,128)S(1)} all-to-all(f32[64,7,2,128]{3,2,1,0:T(2,128)S(1)} %first.1), channel_id=1, replica_groups=mesh['rep'=2,'xh'=2,'zh'=8,'zl'=2,'xl'=2,'y'=4] {'zl','xh','y','rep','xl'}, dimensions={0} | all-to-all | bytes 917504 | tf_op jit(solution)/shard_map/all_to_all | solution.py:314
  27.7 1.1 %second.1 = (f32[288,384]{1,0:T(8,128)S(1)}, f32[24,384]{1,0:T(8,128)S(1)}, f32[24,384]{1,0:T(8,128)S(1)}, f32[8,24,384]{2,1,0:T(8,128)S(1)}) custom-call(f32[64,7,2,128]{3,2,1,0:T(2,128)S(1)} %all_to_all.15.in_ref, f32[24,384]{1,0:T(8,128)S(1)} %add_add_fusion.lam_ref, bf16[384,384]{1,0:T(8,128)(2,1)S(1)} %copy-done, bf16[384,384]{1,0:T(8,128)(2,1)S(1)} %copy-done.1), custom_call_target="tpu_custom_call" | custom-call | tf_op jit(solution)/shard_map/second/pallas_call | solution.py:345
  28.8 27.8 %all_to_all.16.waves_ref = f32[8,24,384]{2,1,0:T(8,128)S(1)} all-to-all(f32[8,24,384]{2,1,0:T(8,128)S(1)} %get-tuple-element.20), channel_id=1, replica_groups={{0,16,32,48,72,88,104,120},{8,24,40,56,64,80,96,112},{1,17,33,49,73,89,..., dimensions={0} | all-to-all | bytes 589824 | tf_op jit(solution)/shard_map/all_to_all | solution.py:319
  56.6 1.3 %third.1 = f32[64,7,2,128]{3,2,1,0:T(2,128)S(1)} custom-call(s32[1]{0:T(128)} %bitcast.7.place_ref, f32[288,384]{1,0:T(8,128)S(1)} %get-tuple-element.17.field_ref, f32[24,384]{1,0:T(8,128)S(1)} %get-tuple-element.18.right_ref, f32[24,384]{1,0:T(8,128)S(1)} %get-tuple-element.19.left_ref, f32[8,24,384]{2,1,0:T(8,128)S(1)} %all_to_all.16.waves_ref, ...), custom_call_target="tpu_custom_call" | custom-call | tf_op jit(solution)/shard_map/third/pallas_call | solution.py:352
  58.0 24.4 %all_to_all.17.in_ref = f32[64,7,2,128]{3,2,1,0:T(2,128)S(1)} all-to-all(f32[64,7,2,128]{3,2,1,0:T(2,128)S(1)} %third.1), channel_id=1, replica_groups=mesh['rep'=2,'xh'=2,'zh'=8,'zl'=2,'xl'=2,'y'=4] {'zl','xh','y','rep','xl'}, dimensions={0} | all-to-all | bytes 917504 | tf_op jit(solution)/shard_map/all_to_all | solution.py:314
  82.4 1.5 %last.1 = f32[12,24,384]{2,1,0:T(8,128)} custom-call(s32[1]{0:T(128)} %bitcast.twist_ref, f32[64,7,2,128]{3,2,1,0:T(2,128)S(1)} %all_to_all.17.in_ref, bf16[384,384]{1,0:T(8,128)(2,1)S(1)} %copy-done, bf16[384,384]{1,0:T(8,128)(2,1)S(1)} %copy-done.1), custom_call_target="tpu_custom_call" | custom-call | tf_op jit(solution)/shard_map/last/pallas_call | solution.py:359
  (1 shorter events, 0.0 us)
Async XLA Ops:
  0.0 9.9 %copy-start.2 = (f32[1,48,12,384]{3,1,2,0:T(8,128)S(1)}, f32[1,48,12,384]{3,1,2,0:T(8,128)}, u32[]{:S(2)}) copy-start(f32[1,48,12,384]{3,1,2,0:T(8,128)} %param.5) | copy-start | bytes 2654212
  1.1 10.2 %collective-permute-start = (f32[12,24,384]{2,1,0:T(8,128)S(1)}, f32[12,24,384]{2,1,0:T(8,128)S(1)}, u32[]{:S(2)}, u32[]{:S(2)}) collective-permute-start(f32[12,24,384]{2,1,0:T(8,128)S(1)} %dynamic-slice_bitcast_fusion), channel_id=1, source_target_pairs={{0,256},{256,0},{1,257},{257,1},{2,258},{258,2},{3,259},{259,3},{4... | collective-permute-start | bytes 1327112 | tf_op jit(solution)/shard_map/ppermute | solution.py:331
  9.9 1.3 %copy-start = (bf16[384,384]{1,0:T(8,128)(2,1)S(1)}, bf16[384,384]{1,0:T(8,128)(2,1)}, u32[]{:S(2)}) copy-start(bf16[384,384]{1,0:T(8,128)(2,1)} %constant.80.clone.high_ref) | copy-start | bytes 884740
  10.0 1.3 %copy-start.1 = (bf16[384,384]{1,0:T(8,128)(2,1)S(1)}, bf16[384,384]{1,0:T(8,128)(2,1)}, u32[]{:S(2)}) copy-start(bf16[384,384]{1,0:T(8,128)(2,1)} %constant.81.clone.low_ref) | copy-start | bytes 884740
  10.0 0.8 copy-start.3

commit v6 on v5

--- a/solution.py
+++ b/solution.py
@@ -20,6 +20,7 @@
 PACKED = 2 * TILES + 1
 PARTS, PAIR = 4, 2
 RING = ROW // PARTS
+ORDER = (4, 0, 5, 1, 6, 2, 7, 3)
 VMEM_BYTES = 12 * 2**20
 F32 = jnp.float32
 BF16 = jnp.bfloat16
@@ -197,7 +198,7 @@
         before, rest, whole, decay = zero, zero, zero, jnp.ones((8, N), F32)
         for k in range(RING):
             member = k if forward else RING - 1 - k
-            wave = waves_ref[member, at, :]
+            wave = waves_ref[ORDER.index(member), at, :]
             earlier = member < place if forward else member > place
             before = jnp.where(earlier, before * pair + wave, before)
             rest = jnp.where(earlier, rest, rest * pair + wave)
@@ -315,7 +316,7 @@
 
 
 def ring_exchange(x):
-    rings = [[2 * k + (half ^ (k // (RING // 2))) for k in range(RING)] for half in range(2)]
+    rings = [[2 * k + (half ^ (k // (RING // 2))) for k in ORDER] for half in range(2)]
     return lax.all_to_all(x, ("zh", "zl"), 0, 0, axis_index_groups=rings, tiled=True)
 
 

time: 84.2 us -> 78.4 us (0.931)
  blocking collectives: 67.7 us -> 61.9 us
    all_to_all x2, blocking collectives: 39.9 us -> 31.5 us  [exchange(): return lax.all_to_all(x, ('zl', 'xh', 'y', 'rep', 'xl'), 0, 0, tiled=True)]
    all_to_all x1, blocking collectives: 27.8 us -> 30.4 us  [ring_exchange(): lax.all_to_all(x, ('zh', 'zl'), 0, 0, axis_index_groups=rings, tiled=True)]
where the time goes in v6:
time: 78.4 us; the launch traced here: 78.2 us
  blocking collectives  61.9 us (79%)
  starting transfers between devices  8.75 us (11%)
  Pallas kernels  4.93 us (6%)
  local copies, waits for them, and re-layouts  1.9 us (2%)
    all_to_all x2, blocking collectives, exchange(): return lax.all_to_all(x, ('zl', 'xh', 'y', 'rep', 'xl'), 0, 0, tiled=True)  31.5 us
    all_to_all x1, blocking collectives, ring_exchange(): lax.all_to_all(x, ('zh', 'zl'), 0, 0, axis_index_groups=rings, tiled=True)  30.4 us
    ppermute x1, starting transfers between devices, body(): got = lax.ppermute(other, 'rep', [(0, 1), (1, 0)])  8.75 us
  transfers between devices with their start and end apart: 1, of which 1 were waited for; matrix products, arithmetic and copies ran while one was open for 1% of the time, Pallas kernels for 0%

profile of v6, /device:TPU:1, one launch (start us, length us, event | category | flops | bytes accessed | tf_op | source)
XLA Modules:
  0.0 78.2 jit_solution(12557075315242473168)
XLA Ops:
  0.0 0.0 copy-start.2
  0.0 1.1 %dynamic-slice_bitcast_fusion = f32[12,24,384]{2,1,0:T(8,128)S(1)} fusion(f32[1,48,12,384]{3,1,2,0:T(8,128)} %param.5, s32[]{:T(128)S(6)} %select_n.22), kind=kLoop, calls=%fused_computation | loop fusion | bytes 884740 | tf_op jit(solution)/shard_map/dynamic_slice | solution.py:331
  1.1 8.7 %collective-permute-start = (f32[12,24,384]{2,1,0:T(8,128)S(1)}, f32[12,24,384]{2,1,0:T(8,128)S(1)}, u32[]{:S(2)}, u32[]{:S(2)}) collective-permute-start(f32[12,24,384]{2,1,0:T(8,128)S(1)} %dynamic-slice_bitcast_fusion), channel_id=1, source_target_pairs={{0,256},{256,0},{1,257},{257,1},{2,258},{258,2},{3,259},{259,3},{4... | collective-permute-start | bytes 1327112 | tf_op jit(solution)/shard_map/ppermute | solution.py:332
  9.9 0.0 copy-done.2
  9.9 0.0 copy-start
  10.0 0.0 copy-start.1
  10.0 0.0 copy-start.3
  10.0 0.8 dynamic-slice_bitcast_fusion.1
  10.8 0.0 copy-done.3
  10.8 0.1 add_add_fusion.lam_ref
  10.9 0.4 collective-permute-done.got_ref
  11.3 0.0 copy-done
  11.3 0.0 copy-done.1
  11.3 1.0 %first.1 = f32[64,7,2,128]{3,2,1,0:T(2,128)S(1)} custom-call(s32[1]{0:T(128)} %bitcast.twist_ref, f32[12,24,384]{2,1,0:T(8,128)S(1)} %mine.1.mine_ref, f32[12,24,384]{2,1,0:T(8,128)S(1)} %collective-permute-done.got_ref, bf16[384,384]{1,0:T(8,128)(2,1)S(1)} %copy-done, bf16[384,384]{1,0:T(8,128)(2,1)S(1)} %copy-done.1), custom_call_target="tpu_custom_call" | custom-call | tf_op jit(solution)/shard_map/first/pallas_call | solution.py:341
  12.3 15.4 %all_to_all.15.in_ref = f32[64,7,2,128]{3,2,1,0:T(2,128)S(1)} all-to-all(f32[64,7,2,128]{3,2,1,0:T(2,128)S(1)} %first.1), channel_id=1, replica_groups=mesh['rep'=2,'xh'=2,'zh'=8,'zl'=2,'xl'=2,'y'=4] {'zl','xh','y','rep','xl'}, dimensions={0} | all-to-all | bytes 917504 | tf_op jit(solution)/shard_map/all_to_all | solution.py:315
  27.7 1.1 %second.1 = (f32[288,384]{1,0:T(8,128)S(1)}, f32[24,384]{1,0:T(8,128)S(1)}, f32[24,384]{1,0:T(8,128)S(1)}, f32[8,24,384]{2,1,0:T(8,128)S(1)}) custom-call(f32[64,7,2,128]{3,2,1,0:T(2,128)S(1)} %all_to_all.15.in_ref, f32[24,384]{1,0:T(8,128)S(1)} %add_add_fusion.lam_ref, bf16[384,384]{1,0:T(8,128)(2,1)S(1)} %copy-done, bf16[384,384]{1,0:T(8,128)(2,1)S(1)} %copy-done.1), custom_call_target="tpu_custom_call" | custom-call | tf_op jit(solution)/shard_map/second/pallas_call | solution.py:346
  28.8 30.4 %all_to_all.16.waves_ref = f32[8,24,384]{2,1,0:T(8,128)S(1)} all-to-all(f32[8,24,384]{2,1,0:T(8,128)S(1)} %get-tuple-element.20), channel_id=1, replica_groups={{72,0,88,16,104,32,120,48},{64,8,80,24,96,40,112,56},{73,1,89,17,105,33..., dimensions={0} | all-to-all | bytes 589824 | tf_op jit(solution)/shard_map/all_to_all | solution.py:320
  59.2 1.3 %third.1 = f32[64,7,2,128]{3,2,1,0:T(2,128)S(1)} custom-call(s32[1]{0:T(128)} %bitcast.7.place_ref, f32[288,384]{1,0:T(8,128)S(1)} %get-tuple-element.17.field_ref, f32[24,384]{1,0:T(8,128)S(1)} %get-tuple-element.18.right_ref, f32[24,384]{1,0:T(8,128)S(1)} %get-tuple-element.19.left_ref, f32[8,24,384]{2,1,0:T(8,128)S(1)} %all_to_all.16.waves_ref, ...), custom_call_target="tpu_custom_call" | custom-call | tf_op jit(solution)/shard_map/third/pallas_call | solution.py:353
  60.5 16.1 %all_to_all.17.in_ref = f32[64,7,2,128]{3,2,1,0:T(2,128)S(1)} all-to-all(f32[64,7,2,128]{3,2,1,0:T(2,128)S(1)} %third.1), channel_id=1, replica_groups=mesh['rep'=2,'xh'=2,'zh'=8,'zl'=2,'xl'=2,'y'=4] {'zl','xh','y','rep','xl'}, dimensions={0} | all-to-all | bytes 917504 | tf_op jit(solution)/shard_map/all_to_all | solution.py:315
  76.6 1.5 %last.1 = f32[12,24,384]{2,1,0:T(8,128)} custom-call(s32[1]{0:T(128)} %bitcast.twist_ref, f32[64,7,2,128]{3,2,1,0:T(2,128)S(1)} %all_to_all.17.in_ref, bf16[384,384]{1,0:T(8,128)(2,1)S(1)} %copy-done, bf16[384,384]{1,0:T(8,128)(2,1)S(1)} %copy-done.1), custom_call_target="tpu_custom_call" | custom-call | tf_op jit(solution)/shard_map/last/pallas_call | solution.py:360
  (1 shorter events, 0.0 us)
Async XLA Ops:
  0.0 9.9 %copy-start.2 = (f32[1,48,12,384]{3,1,2,0:T(8,128)S(1)}, f32[1,48,12,384]{3,1,2,0:T(8,128)}, u32[]{:S(2)}) copy-start(f32[1,48,12,384]{3,1,2,0:T(8,128)} %param.5) | copy-start | bytes 2654212
  1.1 10.2 %collective-permute-start = (f32[12,24,384]{2,1,0:T(8,128)S(1)}, f32[12,24,384]{2,1,0:T(8,128)S(1)}, u32[]{:S(2)}, u32[]{:S(2)}) collective-permute-start(f32[12,24,384]{2,1,0:T(8,128)S(1)} %dynamic-slice_bitcast_fusion), channel_id=1, source_target_pairs={{0,256},{256,0},{1,257},{257,1},{2,258},{258,2},{3,259},{259,3},{4... | collective-permute-start | bytes 1327112 | tf_op jit(solution)/shard_map/ppermute | solution.py:332
  9.9 1.3 %copy-start = (bf16[384,384]{1,0:T(8,128)(2,1)S(1)}, bf16[384,384]{1,0:T(8,128)(2,1)}, u32[]{:S(2)}) copy-start(bf16[384,384]{1,0:T(8,128)(2,1)} %constant.80.clone.high_ref) | copy-start | bytes 884740
  10.0 1.3 %copy-start.1 = (bf16[384,384]{1,0:T(8,128)(2,1)S(1)}, bf16[384,384]{1,0:T(8,128)(2,1)}, u32[]{:S(2)}) copy-start(bf16[384,384]{1,0:T(8,128)(2,1)} %constant.81.clone.low_ref) | copy-start | bytes 884740
  10.0 0.8 copy-start.3

commit v7 on v6

--- a/solution.py
+++ b/solution.py
@@ -20,7 +20,7 @@
 PACKED = 2 * TILES + 1
 PARTS, PAIR = 4, 2
 RING = ROW // PARTS
-ORDER = (4, 0, 5, 1, 6, 2, 7, 3)
+ORDER = (4, 1, 5, 0, 6, 2, 3, 7)
 VMEM_BYTES = 12 * 2**20
 F32 = jnp.float32
 BF16 = jnp.bfloat16

time: 78.4 us -> 78.3 us (level)
  no operation moved by 1% of the time
where the time goes in v7:
time: 78.3 us; the launch traced here: 78 us
  blocking collectives  61.8 us (79%)
  starting transfers between devices  8.75 us (11%)
  Pallas kernels  4.93 us (6%)
  local copies, waits for them, and re-layouts  1.9 us (2%)
    all_to_all x2, blocking collectives, exchange(): return lax.all_to_all(x, ('zl', 'xh', 'y', 'rep', 'xl'), 0, 0, tiled=True)  31.6 us
    all_to_all x1, blocking collectives, ring_exchange(): lax.all_to_all(x, ('zh', 'zl'), 0, 0, axis_index_groups=rings, tiled=True)  30.2 us
    ppermute x1, starting transfers between devices, body(): got = lax.ppermute(other, 'rep', [(0, 1), (1, 0)])  8.75 us
  transfers between devices with their start and end apart: 1, of which 1 were waited for; matrix products, arithmetic and copies ran while one was open for 1% of the time, Pallas kernels for 0%

profile of v7, /device:TPU:1, one launch (start us, length us, event | category | flops | bytes accessed | tf_op | source)
XLA Modules:
  0.0 78.0 jit_solution(14491090136165808024)
XLA Ops:
  0.0 0.0 copy-start.2
  0.0 1.1 %dynamic-slice_bitcast_fusion = f32[12,24,384]{2,1,0:T(8,128)S(1)} fusion(f32[1,48,12,384]{3,1,2,0:T(8,128)} %param.5, s32[]{:T(128)S(6)} %select_n.22), kind=kLoop, calls=%fused_computation | loop fusion | bytes 884740 | tf_op jit(solution)/shard_map/dynamic_slice | solution.py:331
  1.1 8.7 %collective-permute-start = (f32[12,24,384]{2,1,0:T(8,128)S(1)}, f32[12,24,384]{2,1,0:T(8,128)S(1)}, u32[]{:S(2)}, u32[]{:S(2)}) collective-permute-start(f32[12,24,384]{2,1,0:T(8,128)S(1)} %dynamic-slice_bitcast_fusion), channel_id=1, source_target_pairs={{0,256},{256,0},{1,257},{257,1},{2,258},{258,2},{3,259},{259,3},{4... | collective-permute-start | bytes 1327112 | tf_op jit(solution)/shard_map/ppermute | solution.py:332
  9.9 0.0 copy-done.2
  9.9 0.0 copy-start
  10.0 0.0 copy-start.1
  10.0 0.0 copy-start.3
  10.0 0.8 dynamic-slice_bitcast_fusion.1
  10.8 0.0 copy-done.3
  10.8 0.1 add_add_fusion.lam_ref
  10.9 0.4 collective-permute-done.got_ref
  11.3 0.0 copy-done
  11.3 0.0 copy-done.1
  11.3 1.0 %first.1 = f32[64,7,2,128]{3,2,1,0:T(2,128)S(1)} custom-call(s32[1]{0:T(128)} %bitcast.twist_ref, f32[12,24,384]{2,1,0:T(8,128)S(1)} %mine.1.mine_ref, f32[12,24,384]{2,1,0:T(8,128)S(1)} %collective-permute-done.got_ref, bf16[384,384]{1,0:T(8,128)(2,1)S(1)} %copy-done, bf16[384,384]{1,0:T(8,128)(2,1)S(1)} %copy-done.1), custom_call_target="tpu_custom_call" | custom-call | tf_op jit(solution)/shard_map/first/pallas_call | solution.py:341
  12.3 15.4 %all_to_all.15.in_ref = f32[64,7,2,128]{3,2,1,0:T(2,128)S(1)} all-to-all(f32[64,7,2,128]{3,2,1,0:T(2,128)S(1)} %first.1), channel_id=1, replica_groups=mesh['rep'=2,'xh'=2,'zh'=8,'zl'=2,'xl'=2,'y'=4] {'zl','xh','y','rep','xl'}, dimensions={0} | all-to-all | bytes 917504 | tf_op jit(solution)/shard_map/all_to_all | solution.py:315
  27.7 1.1 %second.1 = (f32[288,384]{1,0:T(8,128)S(1)}, f32[24,384]{1,0:T(8,128)S(1)}, f32[24,384]{1,0:T(8,128)S(1)}, f32[8,24,384]{2,1,0:T(8,128)S(1)}) custom-call(f32[64,7,2,128]{3,2,1,0:T(2,128)S(1)} %all_to_all.15.in_ref, f32[24,384]{1,0:T(8,128)S(1)} %add_add_fusion.lam_ref, bf16[384,384]{1,0:T(8,128)(2,1)S(1)} %copy-done, bf16[384,384]{1,0:T(8,128)(2,1)S(1)} %copy-done.1), custom_call_target="tpu_custom_call" | custom-call | tf_op jit(solution)/shard_map/second/pallas_call | solution.py:346
  28.8 30.2 %all_to_all.16.waves_ref = f32[8,24,384]{2,1,0:T(8,128)S(1)} all-to-all(f32[8,24,384]{2,1,0:T(8,128)S(1)} %get-tuple-element.20), channel_id=1, replica_groups={{72,16,88,0,104,32,48,120},{64,24,80,8,96,40,56,112},{73,17,89,1,105,33..., dimensions={0} | all-to-all | bytes 589824 | tf_op jit(solution)/shard_map/all_to_all | solution.py:320
  59.0 1.3 %third.1 = f32[64,7,2,128]{3,2,1,0:T(2,128)S(1)} custom-call(s32[1]{0:T(128)} %bitcast.7.place_ref, f32[288,384]{1,0:T(8,128)S(1)} %get-tuple-element.17.field_ref, f32[24,384]{1,0:T(8,128)S(1)} %get-tuple-element.18.right_ref, f32[24,384]{1,0:T(8,128)S(1)} %get-tuple-element.19.left_ref, f32[8,24,384]{2,1,0:T(8,128)S(1)} %all_to_all.16.waves_ref, ...), custom_call_target="tpu_custom_call" | custom-call | tf_op jit(solution)/shard_map/third/pallas_call | solution.py:353
  60.3 16.1 %all_to_all.17.in_ref = f32[64,7,2,128]{3,2,1,0:T(2,128)S(1)} all-to-all(f32[64,7,2,128]{3,2,1,0:T(2,128)S(1)} %third.1), channel_id=1, replica_groups=mesh['rep'=2,'xh'=2,'zh'=8,'zl'=2,'xl'=2,'y'=4] {'zl','xh','y','rep','xl'}, dimensions={0} | all-to-all | bytes 917504 | tf_op jit(solution)/shard_map/all_to_all | solution.py:315
  76.5 1.5 %last.1 = f32[12,24,384]{2,1,0:T(8,128)} custom-call(s32[1]{0:T(128)} %bitcast.twist_ref, f32[64,7,2,128]{3,2,1,0:T(2,128)S(1)} %all_to_all.17.in_ref, bf16[384,384]{1,0:T(8,128)(2,1)S(1)} %copy-done, bf16[384,384]{1,0:T(8,128)(2,1)S(1)} %copy-done.1), custom_call_target="tpu_custom_call" | custom-call | tf_op jit(solution)/shard_map/last/pallas_call | solution.py:360
  (1 shorter events, 0.0 us)
Async XLA Ops:
  0.0 9.9 %copy-start.2 = (f32[1,48,12,384]{3,1,2,0:T(8,128)S(1)}, f32[1,48,12,384]{3,1,2,0:T(8,128)}, u32[]{:S(2)}) copy-start(f32[1,48,12,384]{3,1,2,0:T(8,128)} %param.5) | copy-start | bytes 2654212
  1.1 10.2 %collective-permute-start = (f32[12,24,384]{2,1,0:T(8,128)S(1)}, f32[12,24,384]{2,1,0:T(8,128)S(1)}, u32[]{:S(2)}, u32[]{:S(2)}) collective-permute-start(f32[12,24,384]{2,1,0:T(8,128)S(1)} %dynamic-slice_bitcast_fusion), channel_id=1, source_target_pairs={{0,256},{256,0},{1,257},{257,1},{2,258},{258,2},{3,259},{259,3},{4... | collective-permute-start | bytes 1327112 | tf_op jit(solution)/shard_map/ppermute | solution.py:332
  9.9 1.3 %copy-start = (bf16[384,384]{1,0:T(8,128)(2,1)S(1)}, bf16[384,384]{1,0:T(8,128)(2,1)}, u32[]{:S(2)}) copy-start(bf16[384,384]{1,0:T(8,128)(2,1)} %constant.80.clone.high_ref) | copy-start | bytes 884740
  10.0 1.3 %copy-start.1 = (bf16[384,384]{1,0:T(8,128)(2,1)S(1)}, bf16[384,384]{1,0:T(8,128)(2,1)}, u32[]{:S(2)}) copy-start(bf16[384,384]{1,0:T(8,128)(2,1)} %constant.81.clone.low_ref) | copy-start | bytes 884740
  10.0 0.8 copy-start.3

commit v8 on v7

--- a/solution.py
+++ b/solution.py
@@ -20,7 +20,7 @@
 PACKED = 2 * TILES + 1
 PARTS, PAIR = 4, 2
 RING = ROW // PARTS
-ORDER = (4, 1, 5, 0, 6, 2, 3, 7)
+ORDER = (4, 0, 1, 5, 6, 2, 3, 7)
 VMEM_BYTES = 12 * 2**20
 F32 = jnp.float32
 BF16 = jnp.bfloat16

time: 78.3 us -> 78.4 us (level)
  no operation moved by 1% of the time
where the time goes in v8:
time: 78.4 us; the launch traced here: 78.1 us
  blocking collectives  61.9 us (79%)
  starting transfers between devices  8.75 us (11%)
  Pallas kernels  4.93 us (6%)
  local copies, waits for them, and re-layouts  1.9 us (2%)
    all_to_all x2, blocking collectives, exchange(): return lax.all_to_all(x, ('zl', 'xh', 'y', 'rep', 'xl'), 0, 0, tiled=True)  31.5 us
    all_to_all x1, blocking collectives, ring_exchange(): lax.all_to_all(x, ('zh', 'zl'), 0, 0, axis_index_groups=rings, tiled=True)  30.4 us
    ppermute x1, starting transfers between devices, body(): got = lax.ppermute(other, 'rep', [(0, 1), (1, 0)])  8.75 us
  transfers between devices with their start and end apart: 1, of which 1 were waited for; matrix products, arithmetic and copies ran while one was open for 1% of the time, Pallas kernels for 0%

profile of v8, /device:TPU:1, one launch (start us, length us, event | category | flops | bytes accessed | tf_op | source)
XLA Modules:
  0.0 78.1 jit_solution(14931706148534231140)
XLA Ops:
  0.0 0.0 copy-start.2
  0.0 1.1 %dynamic-slice_bitcast_fusion = f32[12,24,384]{2,1,0:T(8,128)S(1)} fusion(f32[1,48,12,384]{3,1,2,0:T(8,128)} %param.5, s32[]{:T(128)S(6)} %select_n.22), kind=kLoop, calls=%fused_computation | loop fusion | bytes 884740 | tf_op jit(solution)/shard_map/dynamic_slice | solution.py:331
  1.1 8.7 %collective-permute-start = (f32[12,24,384]{2,1,0:T(8,128)S(1)}, f32[12,24,384]{2,1,0:T(8,128)S(1)}, u32[]{:S(2)}, u32[]{:S(2)}) collective-permute-start(f32[12,24,384]{2,1,0:T(8,128)S(1)} %dynamic-slice_bitcast_fusion), channel_id=1, source_target_pairs={{0,256},{256,0},{1,257},{257,1},{2,258},{258,2},{3,259},{259,3},{4... | collective-permute-start | bytes 1327112 | tf_op jit(solution)/shard_map/ppermute | solution.py:332
  9.9 0.0 copy-done.2
  9.9 0.0 copy-start
  10.0 0.0 copy-start.1
  10.0 0.0 copy-start.3
  10.0 0.8 dynamic-slice_bitcast_fusion.1
  10.8 0.0 copy-done.3
  10.8 0.1 add_add_fusion.lam_ref
  10.9 0.4 collective-permute-done.got_ref
  11.3 0.0 copy-done
  11.3 0.0 copy-done.1
  11.3 1.0 %first.1 = f32[64,7,2,128]{3,2,1,0:T(2,128)S(1)} custom-call(s32[1]{0:T(128)} %bitcast.twist_ref, f32[12,24,384]{2,1,0:T(8,128)S(1)} %mine.1.mine_ref, f32[12,24,384]{2,1,0:T(8,128)S(1)} %collective-permute-done.got_ref, bf16[384,384]{1,0:T(8,128)(2,1)S(1)} %copy-done, bf16[384,384]{1,0:T(8,128)(2,1)S(1)} %copy-done.1), custom_call_target="tpu_custom_call" | custom-call | tf_op jit(solution)/shard_map/first/pallas_call | solution.py:341
  12.3 15.4 %all_to_all.15.in_ref = f32[64,7,2,128]{3,2,1,0:T(2,128)S(1)} all-to-all(f32[64,7,2,128]{3,2,1,0:T(2,128)S(1)} %first.1), channel_id=1, replica_groups=mesh['rep'=2,'xh'=2,'zh'=8,'zl'=2,'xl'=2,'y'=4] {'zl','xh','y','rep','xl'}, dimensions={0} | all-to-all | bytes 917504 | tf_op jit(solution)/shard_map/all_to_all | solution.py:315
  27.7 1.1 %second.1 = (f32[288,384]{1,0:T(8,128)S(1)}, f32[24,384]{1,0:T(8,128)S(1)}, f32[24,384]{1,0:T(8,128)S(1)}, f32[8,24,384]{2,1,0:T(8,128)S(1)}) custom-call(f32[64,7,2,128]{3,2,1,0:T(2,128)S(1)} %all_to_all.15.in_ref, f32[24,384]{1,0:T(8,128)S(1)} %add_add_fusion.lam_ref, bf16[384,384]{1,0:T(8,128)(2,1)S(1)} %copy-done, bf16[384,384]{1,0:T(8,128)(2,1)S(1)} %copy-done.1), custom_call_target="tpu_custom_call" | custom-call | tf_op jit(solution)/shard_map/second/pallas_call | solution.py:346
  28.8 30.4 %all_to_all.16.waves_ref = f32[8,24,384]{2,1,0:T(8,128)S(1)} all-to-all(f32[8,24,384]{2,1,0:T(8,128)S(1)} %get-tuple-element.20), channel_id=1, replica_groups={{72,0,16,88,104,32,48,120},{64,8,24,80,96,40,56,112},{73,1,17,89,105,33..., dimensions={0} | all-to-all | bytes 589824 | tf_op jit(solution)/shard_map/all_to_all | solution.py:320
  59.1 1.3 %third.1 = f32[64,7,2,128]{3,2,1,0:T(2,128)S(1)} custom-call(s32[1]{0:T(128)} %bitcast.7.place_ref, f32[288,384]{1,0:T(8,128)S(1)} %get-tuple-element.17.field_ref, f32[24,384]{1,0:T(8,128)S(1)} %get-tuple-element.18.right_ref, f32[24,384]{1,0:T(8,128)S(1)} %get-tuple-element.19.left_ref, f32[8,24,384]{2,1,0:T(8,128)S(1)} %all_to_all.16.waves_ref, ...), custom_call_target="tpu_custom_call" | custom-call | tf_op jit(solution)/shard_map/third/pallas_call | solution.py:353
  60.5 16.1 %all_to_all.17.in_ref = f32[64,7,2,128]{3,2,1,0:T(2,128)S(1)} all-to-all(f32[64,7,2,128]{3,2,1,0:T(2,128)S(1)} %third.1), channel_id=1, replica_groups=mesh['rep'=2,'xh'=2,'zh'=8,'zl'=2,'xl'=2,'y'=4] {'zl','xh','y','rep','xl'}, dimensions={0} | all-to-all | bytes 917504 | tf_op jit(solution)/shard_map/all_to_all | solution.py:315
  76.6 1.5 %last.1 = f32[12,24,384]{2,1,0:T(8,128)} custom-call(s32[1]{0:T(128)} %bitcast.twist_ref, f32[64,7,2,128]{3,2,1,0:T(2,128)S(1)} %all_to_all.17.in_ref, bf16[384,384]{1,0:T(8,128)(2,1)S(1)} %copy-done, bf16[384,384]{1,0:T(8,128)(2,1)S(1)} %copy-done.1), custom_call_target="tpu_custom_call" | custom-call | tf_op jit(solution)/shard_map/last/pallas_call | solution.py:360
  (1 shorter events, 0.0 us)
Async XLA Ops:
  0.0 9.9 %copy-start.2 = (f32[1,48,12,384]{3,1,2,0:T(8,128)S(1)}, f32[1,48,12,384]{3,1,2,0:T(8,128)}, u32[]{:S(2)}) copy-start(f32[1,48,12,384]{3,1,2,0:T(8,128)} %param.5) | copy-start | bytes 2654212
  1.1 10.2 %collective-permute-start = (f32[12,24,384]{2,1,0:T(8,128)S(1)}, f32[12,24,384]{2,1,0:T(8,128)S(1)}, u32[]{:S(2)}, u32[]{:S(2)}) collective-permute-start(f32[12,24,384]{2,1,0:T(8,128)S(1)} %dynamic-slice_bitcast_fusion), channel_id=1, source_target_pairs={{0,256},{256,0},{1,257},{257,1},{2,258},{258,2},{3,259},{259,3},{4... | collective-permute-start | bytes 1327112 | tf_op jit(solution)/shard_map/ppermute | solution.py:332
  9.9 1.3 %copy-start = (bf16[384,384]{1,0:T(8,128)(2,1)S(1)}, bf16[384,384]{1,0:T(8,128)(2,1)}, u32[]{:S(2)}) copy-start(bf16[384,384]{1,0:T(8,128)(2,1)} %constant.80.clone.high_ref) | copy-start | bytes 884740
  10.0 1.3 %copy-start.1 = (bf16[384,384]{1,0:T(8,128)(2,1)S(1)}, bf16[384,384]{1,0:T(8,128)(2,1)}, u32[]{:S(2)}) copy-start(bf16[384,384]{1,0:T(8,128)(2,1)} %constant.81.clone.low_ref) | copy-start | bytes 884740
  10.0 0.8 copy-start.3
